TPU v7x, 512 devices: a whole 4x4x16 slice. The times are simulated.
512 devices in a mesh: grp: 4 (over y_hi, core), gx: 32 (over y_lo, z), gy: 4 (over x).
Axes of the slice: x: 4, y: 4 (y_hi: 2, y_lo: 2; y = y_hi * 2 + y_lo), z: 16, core: 2. Of those that a mesh axis runs over, the one named last changes fastest.
Arguments:
- sources: float32 [4, 128, 32, 512], P('grp', 'gx', 'gy'), may hold values from -4.5 to 5.5
- diagonal: float32 [128, 32, 512], P('gx', 'gy'), may hold values from 0.02 to 0.3
- coarse_ids: int32 [128, 32, 512], P('gx', 'gy'), may hold values from 0 to 255, as said below
- coarse_inverse: float32 [256, 256], replicated, may hold values from -1 to 3
- omega_rows: float32 [4, 32], replicated, may hold values from -5 to 5
- psi: float32 [32, 128, 32, 512], P(None, 'gx', 'gy', 'grp'), may hold values from -0.00390625 to 0.00390625
- phi: float32 [64, 128, 32, 512], P(None, 'gx', 'gy', 'grp'), may hold values from -0.00390625 to 0.00390625
- xi_cols: float32 [64, 4], replicated, may hold values from -5 to 5
- range_sketch: float32 [32, 128, 32, 512], P(None, 'gx', 'gy', 'grp'), may hold values from -3 to 3
- core_sketch: float32 [64, 64], replicated, may hold values from -2 to 2
Outputs:
- range_new: float32 [32, 128, 32, 512], P(None, 'gx', 'gy', 'grp')
- corange_cols: float32 [32, 4], replicated
- core_new: float32 [64, 64], replicated
Inputs may be any that keep to these rules, and one draw needn't show every extreme that they name: `coarse_ids`: the grid is cut into 4, 4 and 16 non-empty ranges of consecutive cells along the three dimensions; coarse cell (a * 4 + b) * 16 + c is the box of ranges a, b, c.
All inputs are finite; a program needn't handle non-finite values.
Results may differ from a plain program's by a relative error of at most 0.0003.
Values sent between devices are 32-bit elements; how exact they have to be, the bound alone decides.
A program may use at most 64 MiB of HBM per device.

v0:
```python
import functools

import jax
import jax.numpy as jnp
from jax import lax
from jax.sharding import Mesh
from jax.sharding import PartitionSpec as P

OUTER = 2
SWEEPS = 4
XY_CUTS = 4
Z_CUTS = 16
GX_GY = ("gx_0", "gx_1", "gy")
GX = ("gx_0", "gx_1")
GRP = ("grp_0", "grp_1")
GRP_GX_GY = ("grp_0", "grp_1", "gx_0", "gx_1", "gy")


jacobi_weight = 2.0 / 3.0
highest = lax.Precision.HIGHEST


def with_halo(x, sides, width):
    edges = {}
    for axis, dim in sides:
        count, length = (lax.axis_size(axis), x.shape[dim])
        up = [(i, (i + 1) % count) for i in range(count - 1)]
        last = lax.slice_in_dim(x, length - width, length, axis=dim)
        leading = lax.slice_in_dim(x, 0, width, axis=dim)
        edges[dim] = (
            lax.ppermute(last, axis, up),
            lax.ppermute(leading, axis, [(b, a) for a, b in up]),
        )
    done = []
    for _, dim in sides:
        low, high = edges[dim]
        around = [(width, width) if d in done else (0, 0) for d in range(x.ndim)]
        x = jnp.concatenate([jnp.pad(low, around), x, jnp.pad(high, around)], axis=dim)
        done.append(dim)
    return x


def with_halo_2(cells, sides, width):
    for axis, dim in sides:
        count = lax.axis_size(axis)
        ends = count - 1
        head = lax.slice_in_dim(cells, 0, width, axis=dim)
        tail = lax.slice_in_dim(cells, cells.shape[dim] - width, cells.shape[dim], axis=dim)
        cells = jnp.concatenate(
            [
                lax.ppermute(tail, axis, [(i, (i + 1) % count) for i in range(ends)]),
                cells,
                lax.ppermute(head, axis, [((i + 1) % count, i) for i in range(ends)]),
            ],
            axis=dim,
        )
    return cells


def one_axis_at_a_time(x, axes):
    return functools.reduce(lax.psum, axes, x)


def neighbour_image(widened, diagonal):
    center = widened[1:-1, 1:-1]
    beside = widened[2:, 1:-1] + widened[:-2, 1:-1]
    beside = beside + widened[1:-1, 2:] + widened[1:-1, :-2]
    padded = jnp.pad(center, ((0, 0), (0, 0), (1, 1)))
    beside = beside + padded[:, :, 2:] + padded[:, :, :-2]
    return (center, (6.0 + diagonal) * center - beside)


def smooth_once(widened, source, diagonal):
    center, applied = neighbour_image(widened, diagonal)
    return center + jacobi_weight * (source - applied) / (6.0 + diagonal)


def widen_faces(values):
    return with_halo(values, ((GX, 0), ("gy", 1)), 1)


def axis_maps(coarse_ids):
    ranks_x = coarse_ids[:, 0, 0] // (XY_CUTS * Z_CUTS)
    ranks_y = coarse_ids[0, :, 0] // Z_CUTS % XY_CUTS
    ranks_z = coarse_ids[0, 0, :] % Z_CUTS
    cuts_xy = jnp.arange(XY_CUTS, dtype=jnp.int32)
    cuts_z = jnp.arange(Z_CUTS, dtype=jnp.int32)
    map_x = (ranks_x[:, None] == cuts_xy[None, :]).astype(jnp.float32)
    map_y = (ranks_y[:, None] == cuts_xy[None, :]).astype(jnp.float32)
    map_z = (ranks_z[:, None] == cuts_z[None, :]).astype(jnp.float32)
    return (map_x, map_y, map_z)


def restrict(values, maps):
    map_x, map_y, map_z = maps
    rows_x, rows_y, cells_z = values.shape
    along_z = jnp.dot(values.reshape(rows_x * rows_y, cells_z), map_z, precision=highest)
    along_z = along_z.reshape(rows_x, rows_y, Z_CUTS)
    along_y = jnp.einsum("xyc,yb->xbc", along_z, map_y, precision=highest)
    along_x = jnp.einsum("xbc,xa->abc", along_y, map_x, precision=highest)
    return along_x.reshape(-1)


def prolong(correction, maps, extent):
    map_x, map_y, map_z = maps
    boxes = correction.reshape(XY_CUTS, XY_CUTS, Z_CUTS)
    over_x = jnp.einsum("abc,xa->xbc", boxes, map_x, precision=highest)
    over_y = jnp.einsum("xbc,yb->xyc", over_x, map_y, precision=highest)
    spread = jnp.dot(over_y.reshape(extent[0] * extent[1], Z_CUTS), map_z.T, precision=highest)
    return spread.reshape(extent)


def body(
    sources,
    diagonal,
    coarse_ids,
    coarse_inverse,
    omega_rows,
    psi,
    phi,
    xi_cols,
    range_sketch,
    core_sketch,
):
    source = sources[0]
    rows_x, rows_y, cells_z = source.shape
    coarse = coarse_inverse.shape[0]
    total_cells = rows_x * lax.axis_size(GX) * rows_y * lax.axis_size("gy") * cells_z
    scale_factor = coarse / total_cells
    maps = axis_maps(coarse_ids)
    stacked = jnp.stack([source, diagonal])
    margin = with_halo_2(stacked, ((GX, 1), ("gy", 2)), 2)
    place_x = lax.axis_index(GX) * rows_x + jnp.arange(rows_x + 4) - 2
    place_y = lax.axis_index("gy") * rows_y + jnp.arange(rows_y + 4) - 2
    inside_x = ((place_x >= 0) & (place_x < rows_x * lax.axis_size(GX))).astype(jnp.float32)
    inside_y = ((place_y >= 0) & (place_y < rows_y * lax.axis_size("gy"))).astype(jnp.float32)
    inside = inside_x[:, None, None] * inside_y[None, :, None]
    pressure = jnp.zeros_like(source)
    for outer_step in range(OUTER):
        if outer_step == 0:
            residual = source
        else:
            residual = source - neighbour_image(widen_faces(pressure), diagonal)[1]
        coarse_rhs = one_axis_at_a_time(restrict(residual, maps), GX_GY)
        correction = jnp.dot(coarse_inverse, coarse_rhs * scale_factor, precision=highest)
        pressure = pressure + prolong(correction, maps, source.shape)
        for sweep_step in range(SWEEPS // 2):
            widened = with_halo_2(pressure, ((GX, 0), ("gy", 1)), 2)
            halfway = (
                smooth_once(widened, margin[0, 1:-1, 1:-1], margin[1, 1:-1, 1:-1])
                * inside[1:-1, 1:-1]
            )
            pressure = smooth_once(halfway, source, diagonal)
    snapshot = lax.all_to_all(pressure[None], GRP, split_axis=3, concat_axis=0, tiled=True)
    columns = snapshot.reshape(snapshot.shape[0], -1)
    range_flat = range_sketch.reshape(range_sketch.shape[0], -1)
    range_new = range_flat + jnp.einsum("tk,tc->kc", omega_rows, columns, precision=highest)
    corange_part = jnp.einsum(
        "lc,tc->lt", psi.reshape(psi.shape[0], -1), columns, precision=highest
    )
    core_part = jnp.einsum("sc,tc->st", phi.reshape(phi.shape[0], -1), columns, precision=highest)
    corange_cols, core_images = (
        one_axis_at_a_time(corange_part, GRP_GX_GY),
        one_axis_at_a_time(core_part, GRP_GX_GY),
    )
    core_new = core_sketch + jnp.dot(core_images, xi_cols.T, precision=highest)
    return (range_new.reshape(range_sketch.shape), corange_cols, core_new)


def solution(mesh):
    finer = Mesh(
        mesh.devices.reshape(2, 2, 2, 16, mesh.shape["gy"]),
        ("grp_0", "grp_1", "gx_0", "gx_1", "gy"),
    )
    placed = (
        P(GRP, GX, "gy", None),
        P(GX, "gy", None),
        P(GX, "gy", None),
        P(),
        P(),
        P(None, GX, "gy", GRP),
        P(None, GX, "gy", GRP),
        P(),
        P(None, GX, "gy", GRP),
        P(),
    )
    return jax.shard_map(
        body,
        mesh=finer,
        in_specs=placed,
        out_specs=(P(None, GX, "gy", GRP), P(), P()),
        check_vma=False,
    )
```

profile of v0, /device:TPU:2, one launch (start us, length us, event | category | flops | bytes accessed | tf_op | source)
XLA Modules:
  0.0 278.5 jit_solution(15647743445635286583)
XLA Ops:
  4.7 4.9 %psum.112 = f32[256]{0:T(256)S(1)} all-reduce(f32[256]{0:T(256)S(1)} %reshape.211), channel_id=1, replica_groups=mesh['grp_0'=2,'grp_1'=2,'gx_0'=2,'gx_1'=16,'gy'=4] {'gx_0'}, use_global_device_ids=true, to_apply=%region_0.1 | all-reduce | flops 256 | bytes 2048 | tf_op jit(solution)/shard_map/psum | solution.py:61
  9.6 36.5 %psum.113 = f32[256]{0:T(256)S(1)} all-reduce(f32[256]{0:T(256)S(1)} %psum.112), channel_id=1, replica_groups=mesh['grp_0'=2,'grp_1'=2,'gx_0'=2,'gx_1'=16,'gy'=4] {'gx_1'}, use_global_device_ids=true, to_apply=%region_1.2 | all-reduce | flops 256 | bytes 2048 | tf_op jit(solution)/shard_map/psum | solution.py:61
  46.1 8.6 %psum.114 = f32[256]{0:T(256)S(1)} all-reduce(f32[256]{0:T(256)S(1)} %psum.113), channel_id=1, replica_groups=mesh['grp_0'=2,'grp_1'=2,'gx_0'=2,'gx_1'=16,'gy'=4] {'gy'}, use_global_device_ids=true, to_apply=%region_2.3 | all-reduce | flops 256 | bytes 2048 | tf_op jit(solution)/shard_map/psum | solution.py:61
  58.9 4.5 %collective-permute-start.4 = (f32[2,2,8,512]{3,2,1,0:T(8,128)S(1)}, f32[2,2,8,512]{3,2,1,0:T(8,128)S(1)}, u32[]{:S(2)}, u32[]{:S(2)}) collective-permute-start(f32[2,2,8,512]{3,2,1,0:T(8,128)S(1)} %get-tuple-element.24), channel_id=1, source_target_pairs={{0,4},{4,8},{8,12},{12,16},{16,20},{20,24},{24,28},{28,32},{32,36}... | collective-permute-start | bytes 196616 | tf_op jit(solution)/shard_map/ppermute | solution.py:51
  65.0 3.1 %collective-permute-start.2 = (f32[8,2,512]{2,1,0:T(2,128)S(1)}, f32[8,2,512]{2,1,0:T(2,128)S(1)}, u32[]{:S(2)}, u32[]{:S(2)}) collective-permute-start(f32[8,2,512]{2,1,0:T(2,128)S(1)} %get-tuple-element.26), channel_id=1, source_target_pairs={{0,1},{1,2},{2,3},{4,5},{5,6},{6,7},{8,9},{9,10},{10,11},{12,13},{... | collective-permute-start | bytes 98312 | tf_op jit(solution)/shard_map/ppermute | solution.py:51
  68.1 2.7 collective-permute-start.3
  70.9 3.1 %collective-permute-start.6 = (f32[2,8,2,512]{3,2,1,0:T(2,128)S(1)}, f32[2,8,2,512]{3,2,1,0:T(2,128)S(1)}, u32[]{:S(2)}, u32[]{:S(2)}) collective-permute-start(f32[2,8,2,512]{3,2,1,0:T(2,128)S(1)} %get-tuple-element.16), channel_id=1, source_target_pairs={{0,1},{1,2},{2,3},{4,5},{5,6},{6,7},{8,9},{9,10},{10,11},{12,13},{... | collective-permute-start | bytes 196616 | tf_op jit(solution)/shard_map/ppermute | solution.py:51
  74.0 2.7 collective-permute-start.7
  77.1 3.1 %collective-permute-done.7 = f32[2,8,2,512]{3,2,1,0:T(2,128)S(1)} collective-permute-done((f32[2,8,2,512]{3,2,1,0:T(2,128)S(1)}, f32[2,8,2,512]{3,2,1,0:T(2,128)S(1)}, u32[]{:S(2)}, u32[]{:S(2)}) %collective-permute-start.7) | collective-permute-done | bytes 65568 | tf_op jit(solution)/shard_map/ppermute | solution.py:53
  80.6 4.5 %collective-permute-start.8 = (f32[2,8,512]{2,1,0:T(8,128)S(1)}, f32[2,8,512]{2,1,0:T(8,128)S(1)}, u32[]{:S(2)}, u32[]{:S(2)}) collective-permute-start(f32[2,8,512]{2,1,0:T(8,128)S(1)} %get-tuple-element.36), channel_id=1, source_target_pairs={{0,4},{4,8},{8,12},{12,16},{16,20},{20,24},{24,28},{28,32},{32,36}... | collective-permute-start | bytes 98312 | tf_op jit(solution)/shard_map/ppermute | solution.py:51
  86.7 4.2 %collective-permute-done.9 = f32[2,8,512]{2,1,0:T(8,128)S(1)} collective-permute-done((f32[2,8,512]{2,1,0:T(8,128)S(1)}, f32[2,8,512]{2,1,0:T(8,128)S(1)}, u32[]{:S(2)}, u32[]{:S(2)}) %collective-permute-start.9) | collective-permute-done | bytes 32800 | tf_op jit(solution)/shard_map/ppermute | solution.py:53
  93.3 3.6 %collective-permute-start.11 = (f32[8,2,512]{2,1,0:T(2,128)S(1)}, f32[8,2,512]{2,1,0:T(2,128)S(1)}, u32[]{:S(2)}, u32[]{:S(2)}) collective-permute-start(f32[8,2,512]{2,1,0:T(2,128)S(1)} %get-tuple-element.23), channel_id=1, source_target_pairs={{1,0},{2,1},{3,2},{5,4},{6,5},{7,6},{9,8},{10,9},{11,10},{13,12},{... | collective-permute-start | bytes 98312 | tf_op jit(solution)/shard_map/ppermute | solution.py:53
  100.8 4.5 %collective-permute-start.13 = (f32[1,8,512]{2,1,0:T(8,128)S(1)}, f32[1,8,512]{2,1,0:T(8,128)S(1)}, u32[]{:S(2)}, u32[]{:S(2)}) collective-permute-start(f32[1,8,512]{2,1,0:T(8,128)S(1)} %get-tuple-element.34), channel_id=1, source_target_pairs={{0,4},{4,8},{8,12},{12,16},{16,20},{20,24},{24,28},{28,32},{32,36}... | collective-permute-start | bytes 49160 | tf_op jit(solution)/shard_map/ppermute | solution.py:31
  105.4 3.6 %collective-permute-start.14 = (f32[4,1,512]{2,1,0:T(1,128)S(1)}, f32[4,1,512]{2,1,0:T(1,128)S(1)}, u32[]{:S(2)}, u32[]{:S(2)}) collective-permute-start(f32[4,1,512]{2,1,0:T(1,128)S(1)} %get-tuple-element.32), channel_id=1, source_target_pairs={{1,0},{2,1},{3,2},{5,4},{6,5},{7,6},{9,8},{10,9},{11,10},{13,12},{... | collective-permute-start | bytes 24584 | tf_op jit(solution)/shard_map/ppermute | solution.py:32
  111.3 3.3 %collective-permute-done.15 = f32[4,1,512]{2,1,0:T(1,128)S(1)} collective-permute-done((f32[4,1,512]{2,1,0:T(1,128)S(1)}, f32[4,1,512]{2,1,0:T(1,128)S(1)}, u32[]{:S(2)}, u32[]{:S(2)}) %collective-permute-start.15) | collective-permute-done | bytes 8224 | tf_op jit(solution)/shard_map/ppermute | solution.py:31
  115.3 13.1 %psum.115 = f32[256]{0:T(256)S(1)} all-reduce(f32[256]{0:T(256)S(1)} %reshape.215), channel_id=1, replica_groups=mesh['grp_0'=2,'grp_1'=2,'gx_0'=2,'gx_1'=16,'gy'=4] {'gx_0'}, use_global_device_ids=true, to_apply=%region_3.4 | all-reduce | flops 256 | bytes 2048 | tf_op jit(solution)/shard_map/psum | solution.py:61
  128.4 31.7 %psum.116 = f32[256]{0:T(256)S(1)} all-reduce(f32[256]{0:T(256)S(1)} %psum.115), channel_id=1, replica_groups=mesh['grp_0'=2,'grp_1'=2,'gx_0'=2,'gx_1'=16,'gy'=4] {'gx_1'}, use_global_device_ids=true, to_apply=%region_4.5 | all-reduce | flops 256 | bytes 2048 | tf_op jit(solution)/shard_map/psum | solution.py:61
  160.1 7.5 %psum.117 = f32[256]{0:T(256)S(1)} all-reduce(f32[256]{0:T(256)S(1)} %psum.116), channel_id=1, replica_groups=mesh['grp_0'=2,'grp_1'=2,'gx_0'=2,'gx_1'=16,'gy'=4] {'gy'}, use_global_device_ids=true, to_apply=%region_5.6 | all-reduce | flops 256 | bytes 2048 | tf_op jit(solution)/shard_map/psum | solution.py:61
  171.4 4.2 %collective-permute-done.17 = f32[2,8,512]{2,1,0:T(8,128)S(1)} collective-permute-done((f32[2,8,512]{2,1,0:T(8,128)S(1)}, f32[2,8,512]{2,1,0:T(8,128)S(1)}, u32[]{:S(2)}, u32[]{:S(2)}) %collective-permute-start.17) | collective-permute-done | bytes 32800 | tf_op jit(solution)/shard_map/ppermute | solution.py:53
  175.7 3.0 %collective-permute-start.18 = (f32[8,2,512]{2,1,0:T(2,128)S(1)}, f32[8,2,512]{2,1,0:T(2,128)S(1)}, u32[]{:S(2)}, u32[]{:S(2)}) collective-permute-start(f32[8,2,512]{2,1,0:T(2,128)S(1)} %get-tuple-element.20), channel_id=1, source_target_pairs={{0,1},{1,2},{2,3},{4,5},{5,6},{6,7},{8,9},{9,10},{10,11},{12,13},{... | collective-permute-start | bytes 98312 | tf_op jit(solution)/shard_map/ppermute | solution.py:51
  178.7 2.9 %collective-permute-start.19 = (f32[8,2,512]{2,1,0:T(2,128)S(1)}, f32[8,2,512]{2,1,0:T(2,128)S(1)}, u32[]{:S(2)}, u32[]{:S(2)}) collective-permute-start(f32[8,2,512]{2,1,0:T(2,128)S(1)} %get-tuple-element.21), channel_id=1, source_target_pairs={{1,0},{2,1},{3,2},{5,4},{6,5},{7,6},{9,8},{10,9},{11,10},{13,12},{... | collective-permute-start | bytes 98312 | tf_op jit(solution)/shard_map/ppermute | solution.py:53
  181.5 2.9 %collective-permute-done.19 = f32[8,2,512]{2,1,0:T(2,128)S(1)} collective-permute-done((f32[8,2,512]{2,1,0:T(2,128)S(1)}, f32[8,2,512]{2,1,0:T(2,128)S(1)}, u32[]{:S(2)}, u32[]{:S(2)}) %collective-permute-start.19) | collective-permute-done | bytes 32800 | tf_op jit(solution)/shard_map/ppermute | solution.py:53
  184.9 3.3 %collective-permute-start.20 = (f32[2,8,512]{2,1,0:T(8,128)S(1)}, f32[2,8,512]{2,1,0:T(8,128)S(1)}, u32[]{:S(2)}, u32[]{:S(2)}) collective-permute-start(f32[2,8,512]{2,1,0:T(8,128)S(1)} %get-tuple-element.28), channel_id=1, source_target_pairs={{0,4},{4,8},{8,12},{12,16},{16,20},{20,24},{24,28},{28,32},{32,36}... | collective-permute-start | bytes 98312 | tf_op jit(solution)/shard_map/ppermute | solution.py:51
  189.8 4.2 %collective-permute-done.21 = f32[2,8,512]{2,1,0:T(8,128)S(1)} collective-permute-done((f32[2,8,512]{2,1,0:T(8,128)S(1)}, f32[2,8,512]{2,1,0:T(8,128)S(1)}, u32[]{:S(2)}, u32[]{:S(2)}) %collective-permute-start.21) | collective-permute-done | bytes 32800 | tf_op jit(solution)/shard_map/ppermute | solution.py:53
  194.1 2.3 collective-permute-start.22
  196.4 3.5 %collective-permute-start.23 = (f32[8,2,512]{2,1,0:T(2,128)S(1)}, f32[8,2,512]{2,1,0:T(2,128)S(1)}, u32[]{:S(2)}, u32[]{:S(2)}) collective-permute-start(f32[8,2,512]{2,1,0:T(2,128)S(1)} %get-tuple-element.19), channel_id=1, source_target_pairs={{1,0},{2,1},{3,2},{5,4},{6,5},{7,6},{9,8},{10,9},{11,10},{13,12},{... | collective-permute-start | bytes 98312 | tf_op jit(solution)/shard_map/ppermute | solution.py:53
  204.2 9.6 %all_to_all.15 = f32[4,1,4096]{2,1,0:T(1,128)S(1)} all-to-all(f32[4,1,4096]{2,1,0:T(1,128)S(1)} %reshape.232), channel_id=1, replica_groups=mesh['grp_0'=2,'grp_1'=2,'gx_0'=2,'gx_1'=16,'gy'=4] {'grp_0','grp_1'}, dimensions={0} | all-to-all | bytes 131072 | tf_op jit(solution)/shard_map/all_to_all | solution.py:154
  220.7 6.5 %all-reduce.15 = (f32[32,4]{0,1:T(4,128)S(1)}, f32[64,4]{0,1:T(4,128)S(1)}) all-reduce(f32[32,4]{0,1:T(4,128)S(1)} %convolution_bitcast_fusion.6, f32[64,4]{0,1:T(4,128)S(1)} %convolution_bitcast_fusion.7), channel_id=1, replica_groups=mesh['grp_0'=2,'grp_1'=2,'gx_0'=2,'gx_1'=16,'gy'=4] {'grp_0'}, use_global_device_ids=true, to_apply=%region_6.7 | all-reduce | flops 384 | bytes 3072 | tf_op jit(solution)/shard_map/psum | solution.py:61
  227.2 2.4 all-reduce.14
  229.7 5.4 %all-reduce.13 = (f32[32,4]{0,1:T(4,128)S(1)}, f32[64,4]{0,1:T(4,128)S(1)}) all-reduce(f32[32,4]{0,1:T(4,128)S(1)} %get-tuple-element.9, f32[64,4]{0,1:T(4,128)S(1)} %get-tuple-element.10), channel_id=1, replica_groups=mesh['grp_0'=2,'grp_1'=2,'gx_0'=2,'gx_1'=16,'gy'=4] {'gx_0'}, use_global_device_ids=true, to_apply=%region_8.9 | all-reduce | flops 384 | bytes 3072 | tf_op jit(solution)/shard_map/psum | solution.py:61
  235.1 32.6 %all-reduce.11 = (f32[32,4]{0,1:T(4,128)S(1)}, f32[64,4]{0,1:T(4,128)S(1)}) all-reduce(f32[32,4]{0,1:T(4,128)S(1)} %get-tuple-element.7, f32[64,4]{0,1:T(4,128)S(1)} %get-tuple-element.8), channel_id=1, replica_groups=mesh['grp_0'=2,'grp_1'=2,'gx_0'=2,'gx_1'=16,'gy'=4] {'gx_1'}, use_global_device_ids=true, to_apply=%region_9.10 | all-reduce | flops 384 | bytes 3072 | tf_op jit(solution)/shard_map/psum | solution.py:61
  267.7 10.0 %all-reduce.12 = (f32[32,4]{0,1:T(4,128)}, f32[64,4]{0,1:T(4,128)S(1)}) all-reduce(f32[32,4]{0,1:T(4,128)S(1)} %get-tuple-element.3, f32[64,4]{0,1:T(4,128)S(1)} %get-tuple-element.4), channel_id=1, replica_groups=mesh['grp_0'=2,'grp_1'=2,'gx_0'=2,'gx_1'=16,'gy'=4] {'gy'}, use_global_device_ids=true, to_apply=%region_10.11 | all-reduce | flops 384 | bytes 3072 | tf_op jit(solution)/shard_map/psum | solution.py:61
  (123 shorter events, 38.9 us)
Async XLA Ops:
  0.6 54.1 %copy-start = (f32[256,256]{1,0:T(8,128)S(1)}, f32[256,256]{1,0:T(8,128)}, u32[]{:S(2)}) copy-start(f32[256,256]{1,0:T(8,128)} %param.13) | copy-start | bytes 786436
  55.7 3.2 %copy-start.1 = (f32[1,4,8,512]{3,2,1,0:T(8,128)S(1)}, f32[1,4,8,512]{3,2,1,0:T(8,128)}, u32[]{:S(2)}) copy-start(f32[1,4,8,512]{3,2,1,0:T(8,128)} %param.10) | copy-start | bytes 196612
  55.7 3.2 %copy-start.2 = (f32[4,8,512]{2,1,0:T(8,128)S(1)}, f32[4,8,512]{2,1,0:T(8,128)}, u32[]{:S(2)}) copy-start(f32[4,8,512]{2,1,0:T(8,128)} %param.11) | copy-start | bytes 196612
  55.7 9.2 %collective-permute-start = (f32[2,8,512]{2,1,0:T(8,128)S(1)}, f32[2,8,512]{2,1,0:T(8,128)S(1)}, u32[]{:S(2)}, u32[]{:S(2)}) collective-permute-start(f32[2,8,512]{2,1,0:T(8,128)S(1)} %get-tuple-element.38), channel_id=1, source_target_pairs={{0,4},{4,8},{8,12},{12,16},{16,20},{20,24},{24,28},{28,32},{32,36}... | collective-permute-start | bytes 98312 | tf_op jit(solution)/shard_map/ppermute | solution.py:51
  57.6 7.4 %collective-permute-start.1 = (f32[2,8,512]{2,1,0:T(8,128)S(1)}, f32[2,8,512]{2,1,0:T(8,128)S(1)}, u32[]{:S(2)}, u32[]{:S(2)}) collective-permute-start(f32[2,8,512]{2,1,0:T(8,128)S(1)} %get-tuple-element.39), channel_id=1, source_target_pairs={{4,0},{8,4},{12,8},{16,12},{20,16},{24,20},{28,24},{32,28},{36,32}... | collective-permute-start | bytes 98312 | tf_op jit(solution)/shard_map/ppermute | solution.py:53
  58.9 11.9 %collective-permute-start.4 = (f32[2,2,8,512]{3,2,1,0:T(8,128)S(1)}, f32[2,2,8,512]{3,2,1,0:T(8,128)S(1)}, u32[]{:S(2)}, u32[]{:S(2)}) collective-permute-start(f32[2,2,8,512]{3,2,1,0:T(8,128)S(1)} %get-tuple-element.24), channel_id=1, source_target_pairs={{0,4},{4,8},{8,12},{12,16},{16,20},{20,24},{24,28},{28,32},{32,36}... | collective-permute-start | bytes 196616 | tf_op jit(solution)/shard_map/ppermute | solution.py:51
  63.5 7.4 %collective-permute-start.5 = (f32[2,2,8,512]{3,2,1,0:T(8,128)S(1)}, f32[2,2,8,512]{3,2,1,0:T(8,128)S(1)}, u32[]{:S(2)}, u32[]{:S(2)}) collective-permute-start(f32[2,2,8,512]{3,2,1,0:T(8,128)S(1)} %get-tuple-element.25), channel_id=1, source_target_pairs={{4,0},{8,4},{12,8},{16,12},{20,16},{24,20},{28,24},{32,28},{36,32}... | collective-permute-start | bytes 196616 | tf_op jit(solution)/shard_map/ppermute | solution.py:53
  65.0 11.8 %collective-permute-start.2 = (f32[8,2,512]{2,1,0:T(2,128)S(1)}, f32[8,2,512]{2,1,0:T(2,128)S(1)}, u32[]{:S(2)}, u32[]{:S(2)}) collective-permute-start(f32[8,2,512]{2,1,0:T(2,128)S(1)} %get-tuple-element.26), channel_id=1, source_target_pairs={{0,1},{1,2},{2,3},{4,5},{5,6},{6,7},{8,9},{9,10},{10,11},{12,13},{... | collective-permute-start | bytes 98312 | tf_op jit(solution)/shard_map/ppermute | solution.py:51
  68.1 8.7 %collective-permute-start.3 = (f32[8,2,512]{2,1,0:T(2,128)S(1)}, f32[8,2,512]{2,1,0:T(2,128)S(1)}, u32[]{:S(2)}, u32[]{:S(2)}) collective-permute-start(f32[8,2,512]{2,1,0:T(2,128)S(1)} %get-tuple-element.27), channel_id=1, source_target_pairs={{1,0},{2,1},{3,2},{5,4},{6,5},{7,6},{9,8},{10,9},{11,10},{13,12},{... | collective-permute-start | bytes 98312 | tf_op jit(solution)/shard_map/ppermute | solution.py:53
  70.9 6.2 %collective-permute-start.6 = (f32[2,8,2,512]{3,2,1,0:T(2,128)S(1)}, f32[2,8,2,512]{3,2,1,0:T(2,128)S(1)}, u32[]{:S(2)}, u32[]{:S(2)}) collective-permute-start(f32[2,8,2,512]{3,2,1,0:T(2,128)S(1)} %get-tuple-element.16), channel_id=1, source_target_pairs={{0,1},{1,2},{2,3},{4,5},{5,6},{6,7},{8,9},{9,10},{10,11},{12,13},{... | collective-permute-start | bytes 196616 | tf_op jit(solution)/shard_map/ppermute | solution.py:51
  74.0 6.2 %collective-permute-start.7 = (f32[2,8,2,512]{3,2,1,0:T(2,128)S(1)}, f32[2,8,2,512]{3,2,1,0:T(2,128)S(1)}, u32[]{:S(2)}, u32[]{:S(2)}) collective-permute-start(f32[2,8,2,512]{3,2,1,0:T(2,128)S(1)} %get-tuple-element.17), channel_id=1, source_target_pairs={{1,0},{2,1},{3,2},{5,4},{6,5},{7,6},{9,8},{10,9},{11,10},{13,12},{... | collective-permute-start | bytes 196616 | tf_op jit(solution)/shard_map/ppermute | solution.py:53
  80.6 6.1 %collective-permute-start.8 = (f32[2,8,512]{2,1,0:T(8,128)S(1)}, f32[2,8,512]{2,1,0:T(8,128)S(1)}, u32[]{:S(2)}, u32[]{:S(2)}) collective-permute-start(f32[2,8,512]{2,1,0:T(8,128)S(1)} %get-tuple-element.36), channel_id=1, source_target_pairs={{0,4},{4,8},{8,12},{12,16},{16,20},{20,24},{24,28},{28,32},{32,36}... | collective-permute-start | bytes 98312 | tf_op jit(solution)/shard_map/ppermute | solution.py:51
  85.2 5.8 %collective-permute-start.9 = (f32[2,8,512]{2,1,0:T(8,128)S(1)}, f32[2,8,512]{2,1,0:T(8,128)S(1)}, u32[]{:S(2)}, u32[]{:S(2)}) collective-permute-start(f32[2,8,512]{2,1,0:T(8,128)S(1)} %get-tuple-element.37), channel_id=1, source_target_pairs={{4,0},{8,4},{12,8},{16,12},{20,16},{24,20},{28,24},{32,28},{36,32}... | collective-permute-start | bytes 98312 | tf_op jit(solution)/shard_map/ppermute | solution.py:53
  91.0 5.9 %collective-permute-start.10 = (f32[8,2,512]{2,1,0:T(2,128)S(1)}, f32[8,2,512]{2,1,0:T(2,128)S(1)}, u32[]{:S(2)}, u32[]{:S(2)}) collective-permute-start(f32[8,2,512]{2,1,0:T(2,128)S(1)} %get-tuple-element.22), channel_id=1, source_target_pairs={{0,1},{1,2},{2,3},{4,5},{5,6},{6,7},{8,9},{9,10},{10,11},{12,13},{... | collective-permute-start | bytes 98312 | tf_op jit(solution)/shard_map/ppermute | solution.py:51
  93.3 5.8 %collective-permute-start.11 = (f32[8,2,512]{2,1,0:T(2,128)S(1)}, f32[8,2,512]{2,1,0:T(2,128)S(1)}, u32[]{:S(2)}, u32[]{:S(2)}) collective-permute-start(f32[8,2,512]{2,1,0:T(2,128)S(1)} %get-tuple-element.23), channel_id=1, source_target_pairs={{1,0},{2,1},{3,2},{5,4},{6,5},{7,6},{9,8},{10,9},{11,10},{13,12},{... | collective-permute-start | bytes 98312 | tf_op jit(solution)/shard_map/ppermute | solution.py:53
  99.5 15.0 %collective-permute-start.12 = (f32[1,8,512]{2,1,0:T(8,128)S(1)}, f32[1,8,512]{2,1,0:T(8,128)S(1)}, u32[]{:S(2)}, u32[]{:S(2)}) collective-permute-start(f32[1,8,512]{2,1,0:T(8,128)S(1)} %get-tuple-element.35), channel_id=1, source_target_pairs={{4,0},{8,4},{12,8},{16,12},{20,16},{24,20},{28,24},{32,28},{36,32}... | collective-permute-start | bytes 49160 | tf_op jit(solution)/shard_map/ppermute | solution.py:32
  100.8 13.7 %collective-permute-start.13 = (f32[1,8,512]{2,1,0:T(8,128)S(1)}, f32[1,8,512]{2,1,0:T(8,128)S(1)}, u32[]{:S(2)}, u32[]{:S(2)}) collective-permute-start(f32[1,8,512]{2,1,0:T(8,128)S(1)} %get-tuple-element.34), channel_id=1, source_target_pairs={{0,4},{4,8},{8,12},{12,16},{16,20},{20,24},{24,28},{28,32},{32,36}... | collective-permute-start | bytes 49160 | tf_op jit(solution)/shard_map/ppermute | solution.py:31
  105.4 5.9 %collective-permute-start.14 = (f32[4,1,512]{2,1,0:T(1,128)S(1)}, f32[4,1,512]{2,1,0:T(1,128)S(1)}, u32[]{:S(2)}, u32[]{:S(2)}) collective-permute-start(f32[4,1,512]{2,1,0:T(1,128)S(1)} %get-tuple-element.32), channel_id=1, source_target_pairs={{1,0},{2,1},{3,2},{5,4},{6,5},{7,6},{9,8},{10,9},{11,10},{13,12},{... | collective-permute-start | bytes 24584 | tf_op jit(solution)/shard_map/ppermute | solution.py:32
  109.0 5.5 %collective-permute-start.15 = (f32[4,1,512]{2,1,0:T(1,128)S(1)}, f32[4,1,512]{2,1,0:T(1,128)S(1)}, u32[]{:S(2)}, u32[]{:S(2)}) collective-permute-start(f32[4,1,512]{2,1,0:T(1,128)S(1)} %get-tuple-element.33), channel_id=1, source_target_pairs={{0,1},{1,2},{2,3},{4,5},{5,6},{6,7},{8,9},{9,10},{10,11},{12,13},{... | collective-permute-start | bytes 24584 | tf_op jit(solution)/shard_map/ppermute | solution.py:31
  168.5 2.9 %collective-permute-start.16 = (f32[2,8,512]{2,1,0:T(8,128)S(1)}, f32[2,8,512]{2,1,0:T(8,128)S(1)}, u32[]{:S(2)}, u32[]{:S(2)}) collective-permute-start(f32[2,8,512]{2,1,0:T(8,128)S(1)} %get-tuple-element.30), channel_id=1, source_target_pairs={{0,4},{4,8},{8,12},{12,16},{16,20},{20,24},{24,28},{28,32},{32,36}... | collective-permute-start | bytes 98312 | tf_op jit(solution)/shard_map/ppermute | solution.py:51
  169.8 5.8 %collective-permute-start.17 = (f32[2,8,512]{2,1,0:T(8,128)S(1)}, f32[2,8,512]{2,1,0:T(8,128)S(1)}, u32[]{:S(2)}, u32[]{:S(2)}) collective-permute-start(f32[2,8,512]{2,1,0:T(8,128)S(1)} %get-tuple-element.31), channel_id=1, source_target_pairs={{4,0},{8,4},{12,8},{16,12},{20,16},{24,20},{28,24},{32,28},{36,32}... | collective-permute-start | bytes 98312 | tf_op jit(solution)/shard_map/ppermute | solution.py:53
  175.7 5.9 %collective-permute-start.18 = (f32[8,2,512]{2,1,0:T(2,128)S(1)}, f32[8,2,512]{2,1,0:T(2,128)S(1)}, u32[]{:S(2)}, u32[]{:S(2)}) collective-permute-start(f32[8,2,512]{2,1,0:T(2,128)S(1)} %get-tuple-element.20), channel_id=1, source_target_pairs={{0,1},{1,2},{2,3},{4,5},{5,6},{6,7},{8,9},{9,10},{10,11},{12,13},{... | collective-permute-start | bytes 98312 | tf_op jit(solution)/shard_map/ppermute | solution.py:51
  178.7 5.8 %collective-permute-start.19 = (f32[8,2,512]{2,1,0:T(2,128)S(1)}, f32[8,2,512]{2,1,0:T(2,128)S(1)}, u32[]{:S(2)}, u32[]{:S(2)}) collective-permute-start(f32[8,2,512]{2,1,0:T(2,128)S(1)} %get-tuple-element.21), channel_id=1, source_target_pairs={{1,0},{2,1},{3,2},{5,4},{6,5},{7,6},{9,8},{10,9},{11,10},{13,12},{... | collective-permute-start | bytes 98312 | tf_op jit(solution)/shard_map/ppermute | solution.py:53
  184.9 4.9 %collective-permute-start.20 = (f32[2,8,512]{2,1,0:T(8,128)S(1)}, f32[2,8,512]{2,1,0:T(8,128)S(1)}, u32[]{:S(2)}, u32[]{:S(2)}) collective-permute-start(f32[2,8,512]{2,1,0:T(8,128)S(1)} %get-tuple-element.28), channel_id=1, source_target_pairs={{0,4},{4,8},{8,12},{12,16},{16,20},{20,24},{24,28},{28,32},{32,36}... | collective-permute-start | bytes 98312 | tf_op jit(solution)/shard_map/ppermute | solution.py:51
  188.3 5.8 %collective-permute-start.21 = (f32[2,8,512]{2,1,0:T(8,128)S(1)}, f32[2,8,512]{2,1,0:T(8,128)S(1)}, u32[]{:S(2)}, u32[]{:S(2)}) collective-permute-start(f32[2,8,512]{2,1,0:T(8,128)S(1)} %get-tuple-element.29), channel_id=1, source_target_pairs={{4,0},{8,4},{12,8},{16,12},{20,16},{24,20},{28,24},{32,28},{36,32}... | collective-permute-start | bytes 98312 | tf_op jit(solution)/shard_map/ppermute | solution.py:53
  194.1 5.9 %collective-permute-start.22 = (f32[8,2,512]{2,1,0:T(2,128)S(1)}, f32[8,2,512]{2,1,0:T(2,128)S(1)}, u32[]{:S(2)}, u32[]{:S(2)}) collective-permute-start(f32[8,2,512]{2,1,0:T(2,128)S(1)} %get-tuple-element.18), channel_id=1, source_target_pairs={{0,1},{1,2},{2,3},{4,5},{5,6},{6,7},{8,9},{9,10},{10,11},{12,13},{... | collective-permute-start | bytes 98312 | tf_op jit(solution)/shard_map/ppermute | solution.py:51
  196.4 5.8 %collective-permute-start.23 = (f32[8,2,512]{2,1,0:T(2,128)S(1)}, f32[8,2,512]{2,1,0:T(2,128)S(1)}, u32[]{:S(2)}, u32[]{:S(2)}) collective-permute-start(f32[8,2,512]{2,1,0:T(2,128)S(1)} %get-tuple-element.19), channel_id=1, source_target_pairs={{1,0},{2,1},{3,2},{5,4},{6,5},{7,6},{9,8},{10,9},{11,10},{13,12},{... | collective-permute-start | bytes 98312 | tf_op jit(solution)/shard_map/ppermute | solution.py:53
  215.1 1.6 copy-start.4
  217.6 1.3 copy-start.5
  217.6 1.3 copy-start.7
  220.7 56.9 %copy-start.6 = (f32[64,64]{1,0:T(8,128)S(1)}, f32[64,64]{1,0:T(8,128)}, u32[]{:S(2)}) copy-start(f32[64,64]{1,0:T(8,128)} %param.19) | copy-start | bytes 49156
  267.7 10.0 %copy-start.8 = (f32[64,4]{0,1:T(4,128)S(1)}, f32[64,4]{0,1:T(4,128)}, u32[]{:S(2)}) copy-start(f32[64,4]{0,1:T(4,128)} %param.17) | copy-start | bytes 3076
  (1 other events, 1.2 us)
where the time goes:
time: 280 us; the launch traced here: 278 us
  blocking collectives  169 us (60%)
  starting transfers between devices  62.9 us (22%)
  waiting for transfers between devices  27.5 us (10%)
  local copies, waits for them, and re-layouts  7.93 us (3%)
  matrix products  7.43 us (3%)
    psum x11, blocking collectives, one_axis_at_a_time(): return functools.reduce(lax.psum, axes, x)  159 us
    ppermute x10, starting transfers between devices, with_halo_2(): lax.ppermute(tail, axis, [(i, (i + 1) % count) for i in range(ends)])  29.3 us
    ppermute x10, waiting for transfers between devices, with_halo_2(): lax.ppermute(head, axis, [((i + 1) % count, i) for i in range(ends)])  23.2 us
    ppermute x10, starting transfers between devices, with_halo_2(): lax.ppermute(head, axis, [((i + 1) % count, i) for i in range(ends)])  21.9 us
    all_to_all x1, blocking collectives, body(): lax.all_to_all(pressure[None], GRP, split_axis=3, concat_axis=0, tiled=True)  9.56 us
    ppermute x2, starting transfers between devices, with_halo(): lax.ppermute(last, axis, up)  6.81 us
  transfers between devices with their start and end apart: 24, of which 12 were waited for; matrix products, arithmetic and copies ran while one was open for 0% of the time, Pallas kernels for 0%

commit v1 on v0

v1 whole, which is shorter than its diff:
```python
import functools

import jax
import jax.numpy as jnp
from jax import lax
from jax.experimental import pallas as pl
from jax.experimental.pallas import tpu as pltpu
from jax.sharding import PartitionSpec as P

OUTER = 2
SWEEPS = 4
XY_CUTS = 4
Z_CUTS = 16
HALO = 4
LANES = 128
THIRD = 1.0 / 3.0
TWO_THIRDS = 2.0 / 3.0

f32 = jnp.float32
bf16 = jnp.bfloat16
MESH = pl.DeviceIdType.MESH
HIGHEST = lax.Precision.HIGHEST
NT = (((1,), (1,)), ((), ()))
NN = (((1,), (0,)), ((), ()))


def dot(a, b, dims, precision=None):
    return lax.dot_general(a, b, dims, precision=precision, preferred_element_type=f32)


def split3(x):
    high = x.astype(bf16)
    rest = x - high.astype(f32)
    middle = rest.astype(bf16)
    low = (rest - middle.astype(f32)).astype(bf16)
    return high, middle, low


def iota(shape, dim):
    return lax.broadcasted_iota(jnp.int32, shape, dim)


def kernel(
    sizes,
    source_ref,
    diagonal_ref,
    ids_ref,
    inverse_ref,
    omega_ref,
    psi_hbm,
    phi_hbm,
    xi_ref,
    range_hbm,
    core_ref,
    range_out,
    corange_out,
    core_out,
    rows_k,
    range_in,
    range_done,
    ext_s,
    ext_d,
    ext_p,
    weight,
    weighted_q,
    field_a,
    field_b,
    final,
    snap,
    packed,
    reduced,
    ranks,
    ranks_in,
    map_zt,
    map_g,
    sum_send,
    zsum,
    psum,
    out_send,
    zout,
    pout,
    local_sem,
    halo_send,
    halo_recv,
    sum_send_sem,
    sum_recv_sem,
    snap_send,
    snap_recv,
):
    n_grp, n_gx, n_gy, n_z, total_cells = sizes
    n_low = n_gx // n_z
    rows_x, rows_y, cells_z = source_ref.shape
    per_k = rows_x * rows_y
    k_psi, k_phi = psi_hbm.shape[0] // per_k, phi_hbm.shape[0] // per_k
    k_all = k_psi + k_phi
    coarse = inverse_ref.shape[0]
    grp, gx, gy = lax.axis_index("grp"), lax.axis_index("gx"), lax.axis_index("gy")
    z_at = lax.rem(gx, n_z)
    low_at = lax.div(gx, n_z)

    z_peers = [
        (grp, low_at * n_z + lax.rem(z_at + i, n_z), gy) for i in range(1, n_z)
    ]
    plane = []
    for i in range(n_grp):
        for j in range(n_low):
            for k in range(n_gy):
                if i or j or k:
                    who = (
                        lax.rem(grp + i, n_grp),
                        lax.rem(gx + j * n_z, n_gx),
                        lax.rem(gy + k, n_gy),
                    )
                    plane.append(((i, j, k), who))
    own_plane = [who for (i, j, k), who in plane if i == 0]
    sides = []
    for ex in (-1, 0, 1):
        for ey in (-1, 0, 1):
            if ex or ey:
                who = (grp, lax.rem(gx + ex + n_gx, n_gx), lax.rem(gy + ey + n_gy, n_gy))
                sides.append(((ex, ey), who))
    everyone = z_peers + [who for _, who in plane] + [who for _, who in sides]
    barrier = pltpu.get_barrier_semaphore()
    for who in everyone:
        pl.semaphore_signal(barrier, inc=1, device_id=who, device_id_type=MESH)

    def remote(src, dst, send, recv, who):
        copy = pltpu.make_async_remote_copy(
            src_ref=src, dst_ref=dst, send_sem=send, recv_sem=recv,
            device_id=who, device_id_type=MESH,
        )
        copy.start()
        return copy

    def wait_bytes(ref, sem):
        pltpu.make_async_copy(ref, ref, sem).wait()

    loads = [
        pltpu.make_async_copy(psi_hbm, rows_k.at[pl.ds(0, k_psi * per_k)], local_sem.at[0]),
        pltpu.make_async_copy(phi_hbm, rows_k.at[pl.ds(k_psi * per_k, k_phi * per_k)], local_sem.at[1]),
        pltpu.make_async_copy(range_hbm, range_in, local_sem.at[2]),
    ]
    for load in loads:
        load.start()

    tile = (rows_y, LANES)
    sub = iota(tile, 0)
    lane = iota(tile, 1)
    box_lane = lane // Z_CUTS
    box = [jnp.broadcast_to(ids_ref[x, :, 0:1] // Z_CUTS, tile) for x in range(rows_x)]
    own_y = (box[0] % XY_CUTS).astype(f32)
    own_x = jnp.zeros(tile, f32)
    for x in range(rows_x):
        own_x = jnp.where(sub == x, (box[x] // XY_CUTS).astype(f32), own_x)
    ranks[0] = own_y
    ranks[1] = own_x
    rank_z = ids_ref[0, 0:1, :] % Z_CUTS
    map_zt[...] = jnp.where(
        iota((LANES, cells_z), 0) % Z_CUTS == rank_z, 1.0, 0.0
    ).astype(bf16)
    map_g[...] = jnp.where(
        iota((coarse, cells_z), 0) % Z_CUTS == rank_z, 1.0, 0.0
    ).astype(bf16)

    def along_z(values):
        parts = dot(jnp.concatenate(split3(values), axis=0), map_zt[...], NT)
        n = values.shape[0]
        return parts[:n] + parts[n : 2 * n] + parts[2 * n :]

    def to_boxes(terms):
        halves = []
        for first in (0, LANES // Z_CUTS):
            total = jnp.zeros(tile, f32)
            for rows, count in terms:
                total = total + rows * count(box_lane + first)
            halves.append(jnp.sum(total, axis=0, keepdims=True))
        return halves

    def same(rank):
        return lambda cell: jnp.where(rank == cell, 1.0, 0.0)

    def start_sum(which, halves):
        for i in range(2):
            sum_send[which, 0, pl.ds(i, 1), :] = halves[i]
        zsum[which, z_at] = sum_send[which, 0]
        for who in z_peers:
            remote(sum_send.at[which, 0], zsum.at[which, z_at],
                   sum_send_sem.at[which, 0], sum_recv_sem.at[which, 0], who)

    def middle_sum(which):
        wait_bytes(zsum.at[which, pl.ds(0, n_z - 1)], sum_recv_sem.at[which, 0])
        total = zsum[which, 0]
        for i in range(1, n_z):
            total = total + zsum[which, i]
        sum_send[which, 1] = total
        at = low_at * n_gy + gy
        psum[which, at] = sum_send[which, 1]
        for who in own_plane:
            remote(sum_send.at[which, 1], psum.at[which, at],
                   sum_send_sem.at[which, 1], sum_recv_sem.at[which, 1], who)

    def end_sum(which):
        n = n_low * n_gy
        wait_bytes(psum.at[which, pl.ds(0, n - 1)], sum_recv_sem.at[which, 1])
        total = psum[which, 0]
        for i in range(1, n):
            total = total + psum[which, i]
        return total * (coarse / total_cells)

    values = along_z(source_ref[...].reshape(per_k, cells_z))
    first_terms = [
        (values[x * rows_y : (x + 1) * rows_y], same(box[x])) for x in range(rows_x)
    ]
    halves = to_boxes(first_terms)

    pl.semaphore_wait(barrier, len(everyone))
    start_sum(0, halves)

    halo_copies = []
    y_from = {-1: pl.ds(0, HALO), 0: pl.ds(0, rows_y), 1: pl.ds(rows_y - HALO, HALO)}
    y_to = {-1: pl.ds(rows_y, HALO), 0: pl.ds(0, rows_y), 1: pl.ds(rows_y + HALO, HALO)}

    def x_rows(ex, depth):
        if ex == 0:
            return 0, HALO, rows_x
        if ex == 1:
            return rows_x - depth, HALO - depth, depth
        return 0, HALO + rows_x, depth

    def send_sides(src, ext, depth, base):
        for n, ((ex, ey), who) in enumerate(sides):
            first, to, count = x_rows(ex, depth - (1 if ex and ey else 0))
            halo_copies.append(
                remote(src.at[pl.ds(first, count), y_from[ey], :],
                       ext.at[pl.ds(to, count), y_to[ey], :],
                       halo_send.at[base + n], halo_recv.at[base + n], who)
            )

    n_rank = 0
    for (ex, ey), who in sides:
        if not (ex and ey):
            halo_copies.append(
                remote(ranks, ranks_in.at[n_rank],
                       halo_send.at[24 + n_rank], halo_recv.at[24 + n_rank], who)
            )
            n_rank += 1
    send_sides(diagonal_ref, ext_d, HALO - 1, 0)
    send_sides(source_ref, ext_s, HALO - 1, 8)
    ext_d[pl.ds(HALO, rows_x), pl.ds(0, rows_y), :] = diagonal_ref[...]
    ext_s[pl.ds(HALO, rows_x), pl.ds(0, rows_y), :] = source_ref[...]

    middle_sum(0)

    for copy in halo_copies:
        copy.wait_recv()
    far = -100.0
    x_after = jnp.where(gx == n_gx - 1, far, ranks_in[0, 1])
    y_after = jnp.where(gy == n_gy - 1, far, ranks_in[1, 0])
    y_before = jnp.where(gy == 0, far, ranks_in[2, 0])
    x_before = jnp.where(gx == 0, far, ranks_in[3, 1])
    rank_x = []
    for rows in (x_before, own_x, x_after):
        for x in range(rows_x):
            rank_x.append(jnp.broadcast_to(rows[x : x + 1], tile))
    halo_y = jnp.where(sub < HALO, y_after, y_before)
    rank_y = jnp.concatenate([own_y, halo_y], axis=0)
    wide = (2 * rows_y, cells_z)
    n_ext = rows_x + 2 * HALO

    def widen(column):
        return jnp.concatenate([column] * (cells_z // LANES), axis=-1)

    def widen_x(rows):
        rows = widen(rows)
        return jnp.concatenate([rows, rows], axis=0)

    rank_y_wide = widen(rank_y)
    rank_x_wide = [widen_x(rows) for rows in rank_x]
    for r in range(1, n_ext - 1):
        here = (rank_x_wide[r] >= 0.0) & (rank_y_wide >= 0.0)
        w = jnp.where(here, TWO_THIRDS / (6.0 + ext_d[r]), 0.0)
        weight[r] = w
        weighted_q[r] = jnp.where(here, w * ext_s[r], 0.0)

    y_up = pltpu.roll(rank_y, 2 * rows_y - 1, 0)[:rows_y]
    y_down = pltpu.roll(rank_y, 1, 0)[:rows_y]

    def beside(x):
        r = HALO + x
        ranks_of = [
            rank_x[r - 1] * XY_CUTS + own_y,
            rank_x[r + 1] * XY_CUTS + own_y,
            rank_x[r] * XY_CUTS + y_up,
            rank_x[r] * XY_CUTS + y_down,
        ]

        def count(cell):
            cell = cell.astype(f32)
            return sum(jnp.where(rank == cell, 1.0, 0.0) for rank in ranks_of)

        return count

    z_lane = iota(wide, 1)

    def z_pair(values, z_lane):
        before = jnp.where(z_lane == 0, 0.0, pltpu.roll(values, 1, 1))
        after = jnp.where(z_lane == cells_z - 1, 0.0, pltpu.roll(values, cells_z - 1, 1))
        return before + after

    def correct(which, store):
        rhs = end_sum(which)
        top = jnp.broadcast_to(rhs[0:1], (8, LANES))
        bottom = jnp.broadcast_to(rhs[1:2], (8, LANES))
        solved = dot(top, inverse_ref[:, 0:LANES], NT, HIGHEST)
        solved = solved + dot(bottom, inverse_ref[:, LANES:], NT, HIGHEST)
        pairs = XY_CUTS * XY_CUTS
        row = iota((pairs, coarse), 0)
        column = iota((pairs, coarse), 1)
        spread = jnp.where(
            column // Z_CUTS == row, jnp.broadcast_to(solved[0:1], (pairs, coarse)), 0.0
        )
        parts = dot(jnp.concatenate(split3(spread), axis=0), map_g[...], NN)
        boxes = parts[:pairs] + parts[pairs : 2 * pairs] + parts[2 * pairs :]
        by_x = []
        for a in range(XY_CUTS):
            picked = jnp.zeros(wide, f32)
            for b in range(XY_CUTS):
                line = boxes[a * XY_CUTS + b : a * XY_CUTS + b + 1]
                picked = jnp.where(rank_y_wide == float(b), jnp.broadcast_to(line, wide), picked)
            by_x.append(picked)
        for r in range(n_ext):
            picked = jnp.zeros(wide, f32)
            for a in range(XY_CUTS):
                picked = jnp.where(rank_x_wide[r] == float(a), by_x[a], picked)
            store(r, picked)

    def sweep(old, new, r):
        here = old[r]
        around = old[r - 1] + old[r + 1]
        around = around + pltpu.roll(here, 1, 0) + pltpu.roll(here, 2 * rows_y - 1, 0)
        around = around + z_pair(here, z_lane)
        new[r] = here * THIRD + weighted_q[r] + weight[r] * around

    def smooth(last):
        fields = (field_a, field_b)
        for s in range(SWEEPS):
            for r in range(1 + s, n_ext - 1 - s):
                if s == SWEEPS - 1:
                    last(r, fields[s % 2])
                else:
                    sweep(fields[s % 2], fields[1 - s % 2], r)

    own_lane = iota((rows_y, cells_z), 1)

    def last_value(r, old):
        here = old[r]
        around = old[r - 1, pl.ds(0, rows_y), :] + old[r + 1, pl.ds(0, rows_y), :]
        beside_y = pltpu.roll(here, 1, 0) + pltpu.roll(here, 2 * rows_y - 1, 0)
        here = here[:rows_y]
        around = around + beside_y[:rows_y] + z_pair(here, own_lane)
        own = pl.ds(0, rows_y)
        return here * THIRD + weighted_q[r, own, :] + weight[r, own, :] * around

    def store_first(r, picked):
        field_a[r] = picked

    correct(0, store_first)

    def last_first(r, old):
        ext_p[r, pl.ds(0, rows_y), :] = last_value(r, old)

    smooth(last_first)

    terms, stack = [], []
    for x in range(rows_x):
        p = ext_p[HALO + x, pl.ds(0, rows_y), :]
        stack.append(source_ref[x] - (6.0 + diagonal_ref[x]) * p + z_pair(p, own_lane))
    for x in range(rows_x):
        stack.append(ext_p[HALO + x, pl.ds(0, rows_y), :])
    values = along_z(jnp.concatenate(stack, axis=0))
    for x in range(2 * rows_x):
        count = same(box[x]) if x < rows_x else beside(x - rows_x)
        terms.append((values[x * rows_y : (x + 1) * rows_y], count))
    start_sum(1, to_boxes(terms))
    pressure_copies = len(halo_copies)
    send_sides(ext_p.at[pl.ds(HALO, rows_x), pl.ds(0, rows_y), :], ext_p, HALO, 16)

    for load in loads[:2]:
        load.wait()

    def pack(at, carry):
        for kt in range(k_all // 8):
            packed[kt, at] = rows_k[pl.ds(kt * 8 * per_k + at, 8, stride=per_k), :]
        return carry

    lax.fori_loop(0, per_k, pack, 0)
    middle_sum(1)
    for copy in halo_copies[pressure_copies:]:
        copy.wait_recv()

    def store_second(r, picked):
        here = (rank_x_wide[r] >= 0.0) & (rank_y_wide >= 0.0)
        field_a[r] = picked + jnp.where(here, ext_p[r], 0.0)

    correct(1, store_second)

    def last_second(r, old):
        final[pl.ds((r - HALO) * rows_y, rows_y), :] = last_value(r, old)

    smooth(last_second)

    snap_copies = []
    own_cells = pl.ds(pl.multiple_of(grp * per_k, per_k), per_k)
    for i in range(1, n_grp):
        other = lax.rem(grp + i, n_grp)
        lanes = pl.ds(pl.multiple_of(other * LANES, LANES), LANES)
        snap_copies.append(
            remote(final.at[:, lanes], snap.at[own_cells],
                   snap_send.at[i - 1], snap_recv.at[0], (other, gx, gy))
        )
    own_lanes = pl.ds(pl.multiple_of(grp * LANES, LANES), LANES)
    snap[own_cells, :] = final[:, own_lanes]
    wait_bytes(snap.at[pl.ds(0, (n_grp - 1) * per_k)], snap_recv.at[0])

    group = 6
    for base in range(0, k_all // 8, group):

        def step(at, carry):
            rows = [
                jnp.broadcast_to(snap[pl.ds(t * per_k + at, 1), :], (8, LANES))
                for t in range(n_grp)
            ]
            out = []
            for n in range(group):
                taken = packed[base + n, at]
                for t in range(n_grp):
                    out.append(carry[n * n_grp + t] + taken * rows[t])
            return tuple(out)

        zeros = tuple(jnp.zeros((8, LANES), f32) for _ in range(group * n_grp))
        sums = lax.fori_loop(0, per_k, step, zeros)
        for n in range(group):
            for t in range(n_grp):
                reduced[pl.ds(t * k_all + (base + n) * 8, 8), :] = sums[n * n_grp + t]
    sums = dot(jnp.ones((8, LANES), f32), reduced[...], NT, HIGHEST)[0:1]
    n_out = n_grp * k_all
    for i in range(n_out // LANES):
        out_send[0, pl.ds(i, 1), :] = sums[:, i * LANES : (i + 1) * LANES]
    for i in range(n_out // LANES, 4):
        out_send[0, pl.ds(i, 1), :] = jnp.zeros((1, LANES), f32)
    zout[z_at] = out_send[0]
    for who in z_peers:
        remote(out_send.at[0], zout.at[z_at], sum_send_sem.at[2, 0], sum_recv_sem.at[2, 0], who)

    loads[2].wait()

    def add_range(k, carry):
        total = range_in[k]
        for t in range(n_grp):
            total = total + omega_ref[t, k] * snap[pl.ds(t * per_k, per_k), :]
        range_done[k] = total
        return carry

    lax.fori_loop(0, range_in.shape[0], add_range, 0)
    store = pltpu.make_async_copy(range_done, range_out, local_sem.at[3])
    store.start()

    wait_bytes(zout.at[pl.ds(0, n_z - 1)], sum_recv_sem.at[2, 0])
    total = zout[0]
    for i in range(1, n_z):
        total = total + zout[i]
    out_send[1] = total
    at = (grp * n_low + low_at) * n_gy + gy
    pout[at] = out_send[1]
    for _, who in plane:
        remote(out_send.at[1], pout.at[at], sum_send_sem.at[2, 1], sum_recv_sem.at[2, 1], who)

    n_core = core_ref.shape[0]
    which_t = iota((n_out, LANES), 0) // k_all
    right = jnp.where(which_t == iota((n_out, LANES), 1) - n_core, 1.0, 0.0)
    lane_t = iota((n_out, 8), 1)
    pick = jnp.where(iota((n_out, 8), 0) // k_all == lane_t, 1.0, 0.0)
    xi = jnp.concatenate([xi_ref[...], jnp.zeros((n_core, 8 - n_grp), f32)], axis=1)
    xi = jnp.concatenate([xi, jnp.zeros((LANES - n_core, 8), f32)], axis=0)
    right = right + dot(pick, xi, NT, HIGHEST)
    left_row = iota((k_all, n_out), 0)
    left_pick = iota((k_all, n_out), 1) % k_all == left_row

    n_plane = n_grp * n_low * n_gy
    wait_bytes(pout.at[pl.ds(0, n_plane - 1)], sum_recv_sem.at[2, 1])
    total = pout[0]
    for i in range(1, n_plane):
        total = total + pout[i]
    line = jnp.concatenate([total[i : i + 1] for i in range(n_out // LANES)], axis=1)
    left = jnp.where(left_pick, jnp.broadcast_to(line, (k_all, n_out)), 0.0)
    result = dot(left, right, NN, HIGHEST)
    corange_out[...] = result[:k_psi, n_core : n_core + n_grp]
    core_out[...] = core_ref[...] + result[k_psi:, :n_core]

    store.wait()
    for copy in halo_copies:
        copy.wait_send()
    for copy in snap_copies:
        copy.wait_send()
    for which in range(2):
        wait_bytes(zsum.at[which, pl.ds(0, n_z - 1)], sum_send_sem.at[which, 0])
        wait_bytes(psum.at[which, pl.ds(0, n_low * n_gy - 1)], sum_send_sem.at[which, 1])
    wait_bytes(zout.at[pl.ds(0, n_z - 1)], sum_send_sem.at[2, 0])
    wait_bytes(pout.at[pl.ds(0, n_plane - 1)], sum_send_sem.at[2, 1])


def solution(mesh):
    n_grp, n_gx, n_gy = (mesh.shape[name] for name in ("grp", "gx", "gy"))
    n_z = min(16, n_gx // 2)
    n_low = n_gx // n_z

    def body(
        sources,
        diagonal,
        coarse_ids,
        coarse_inverse,
        omega_rows,
        psi,
        phi,
        xi_cols,
        range_sketch,
        core_sketch,
    ):
        _, rows_x, rows_y, cells_z = sources.shape
        total_cells = rows_x * n_gx * rows_y * n_gy * cells_z
        k_psi, k_phi = psi.shape[0], phi.shape[0]
        k_all = k_psi + k_phi
        k_range = range_sketch.shape[0]
        n_ext = rows_x + 2 * HALO
        per_k = rows_x * rows_y
        coarse = coarse_inverse.shape[0]
        vmem = pl.BlockSpec(memory_space=pltpu.VMEM)
        smem = pl.BlockSpec(memory_space=pltpu.SMEM)
        hbm = pl.BlockSpec(memory_space=pl.ANY)
        ext = pltpu.VMEM((n_ext, 2 * rows_y, cells_z), f32)
        call = pl.pallas_call(
            functools.partial(kernel, (n_grp, n_gx, n_gy, n_z, total_cells)),
            out_shape=(
                jax.ShapeDtypeStruct((k_range, per_k, LANES), f32),
                jax.ShapeDtypeStruct((k_psi, n_grp), f32),
                jax.ShapeDtypeStruct(core_sketch.shape, f32),
            ),
            in_specs=[vmem, vmem, vmem, vmem, smem, hbm, hbm, vmem, hbm, vmem],
            out_specs=(hbm, vmem, vmem),
            scratch_shapes=[
                pltpu.VMEM((k_all * per_k, LANES), f32),
                pltpu.VMEM((k_range, per_k, LANES), f32),
                pltpu.VMEM((k_range, per_k, LANES), f32),
                ext,
                ext,
                ext,
                ext,
                ext,
                ext,
                ext,
                pltpu.VMEM((per_k, cells_z), f32),
                pltpu.VMEM((n_grp * per_k, LANES), f32),
                pltpu.VMEM((k_all // 8, per_k, 8, LANES), f32),
                pltpu.VMEM((n_grp * k_all, LANES), f32),
                pltpu.VMEM((2, rows_y, LANES), f32),
                pltpu.VMEM((4, 2, rows_y, LANES), f32),
                pltpu.VMEM((LANES, cells_z), bf16),
                pltpu.VMEM((coarse, cells_z), bf16),
                pltpu.VMEM((2, 2, 2, LANES), f32),
                pltpu.VMEM((2, n_z, 2, LANES), f32),
                pltpu.VMEM((2, n_low * n_gy, 2, LANES), f32),
                pltpu.VMEM((2, 4, LANES), f32),
                pltpu.VMEM((n_z, 4, LANES), f32),
                pltpu.VMEM((n_grp * n_low * n_gy, 4, LANES), f32),
                pltpu.SemaphoreType.DMA((4,)),
                pltpu.SemaphoreType.DMA((28,)),
                pltpu.SemaphoreType.DMA((28,)),
                pltpu.SemaphoreType.DMA((3, 2)),
                pltpu.SemaphoreType.DMA((3, 2)),
                pltpu.SemaphoreType.DMA((n_grp - 1,)),
                pltpu.SemaphoreType.DMA((1,)),
            ],
            compiler_params=pltpu.CompilerParams(
                collective_id=0, has_side_effects=True
            ),
            name="two_level_sketch",
        )
        range_new, corange_cols, core_new = call(
            sources[0],
            diagonal,
            coarse_ids,
            coarse_inverse,
            omega_rows,
            psi.reshape(k_psi * per_k, LANES),
            phi.reshape(k_phi * per_k, LANES),
            xi_cols,
            range_sketch.reshape(k_range, per_k, LANES),
            core_sketch,
        )
        return range_new.reshape(range_sketch.shape), corange_cols, core_new

    return jax.shard_map(
        body,
        mesh=mesh,
        in_specs=(
            P("grp", "gx", "gy", None),
            P("gx", "gy", None),
            P("gx", "gy", None),
            P(),
            P(),
            P(None, "gx", "gy", "grp"),
            P(None, "gx", "gy", "grp"),
            P(),
            P(None, "gx", "gy", "grp"),
            P(),
        ),
        out_specs=(P(None, "gx", "gy", "grp"), P(), P()),
        check_vma=False,
    )
```

time: 280 us -> 66.4 us (0.24)
  the two profiles are of different devices: /device:TPU:2 before, /device:TPU:1 now
where the time goes in v1:
time: 66.4 us; the launch traced here: 66.2 us
  Pallas kernels  60.3 us (91%)
  local copies, waits for them, and re-layouts  5.25 us (8%)
    pallas_call x1, Pallas kernels, body(): call(sources[0], diagonal, coarse_ids, coarse_inverse, omega_rows, psi.re...  60.3 us
    unnamed x8, local copies, waits for them, and re-layouts  5.25 us

profile of v1, /device:TPU:1, one launch (start us, length us, event | category | flops | bytes accessed | tf_op | source)
XLA Modules:
  0.0 66.2 jit_solution(9343624601426707996)
XLA Ops:
  0.6 0.0 copy-start.1
  0.6 0.7 %copy-done.1 = f32[64,4]{0,1:T(4,128)S(1)} copy-done((f32[64,4]{0,1:T(4,128)S(1)}, f32[64,4]{0,1:T(4,128)}, u32[]{:S(2)}) %copy-start.1) | copy-done | bytes 1048
  1.3 0.7 %copy.13.xi_ref = f32[64,4]{1,0:T(8,128)} copy(f32[64,4]{0,1:T(4,128)S(1)} %copy-done.1) | data formatting | bytes 2048 | tf_op args[7]
  2.0 60.3 %two_level_sketch.1 = (f32[32,32,128]{2,1,0:T(8,128)}, f32[32,4]{1,0:T(8,128)}, f32[64,64]{1,0:T(8,128)}) custom-call(f32[4,8,512]{2,1,0:T(8,128)} %bitcast.9, f32[4,8,512]{2,1,0:T(8,128)} %diagonal_ref.1, s32[4,8,512]{2,1,0:T(8,128)} %ids_ref.1, f32[256,256]{1,0:T(8,128)} %inverse_ref.1, f32[4,32]{1,0:T(4,128)} %omega_ref.1, f32[1024,128]{1,0:T(8,128)} %bitcast.7, ...), custom_call_target="tpu_custom_call" | custom-call | tf_op jit(solution)/shard_map/two_level_sketch/pallas_call | solution.py:588
  62.3 1.4 %copy.14 = f32[32,4]{0,1:T(4,128)} copy(f32[32,4]{1,0:T(8,128)} %get-tuple-element.10) | data formatting | bytes 1024
  63.7 0.0 copy-start
  63.7 1.9 %copy.17 = f32[32,4,8,128]{3,2,1,0:T(8,128)} copy(f32[32,4,8,128]{3,2,1,0:T(8,128)} %bitcast.6) | data formatting | bytes 1048576
  65.6 0.0 copy-done
  65.6 0.6 copy.18
Async XLA Ops:
  0.6 0.7 %copy-start.1 = (f32[64,4]{0,1:T(4,128)S(1)}, f32[64,4]{0,1:T(4,128)}, u32[]{:S(2)}) copy-start(f32[64,4]{0,1:T(4,128)} %param.17) | copy-start | bytes 3076
  63.7 1.9 %copy-start = (f32[64,64]{1,0:T(8,128)S(1)}, f32[64,64]{1,0:T(8,128)}, u32[]{:S(2)}) copy-start(f32[64,64]{1,0:T(8,128)} %get-tuple-element.17) | copy-start | bytes 49156

commit v2 on v1

--- a/solution.py
+++ b/solution.py
@@ -42,22 +42,28 @@
 
 def kernel(
     sizes,
+    source_hbm,
+    diagonal_hbm,
+    ids_hbm,
+    inverse_hbm,
+    omega_hbm,
+    psi_hbm,
+    phi_hbm,
+    xi_hbm,
+    range_hbm,
+    core_hbm,
+    range_done,
+    corange_out,
+    core_out,
     source_ref,
     diagonal_ref,
     ids_ref,
     inverse_ref,
     omega_ref,
-    psi_hbm,
-    phi_hbm,
     xi_ref,
-    range_hbm,
     core_ref,
-    range_out,
-    corange_out,
-    core_out,
     rows_k,
     range_in,
-    range_done,
     ext_s,
     ext_d,
     ext_p,
@@ -86,6 +92,7 @@
     sum_recv_sem,
     snap_send,
     snap_recv,
+    chain,
 ):
     n_grp, n_gx, n_gy, n_z, total_cells = sizes
     n_low = n_gx // n_z
@@ -119,9 +126,11 @@
             if ex or ey:
                 who = (grp, lax.rem(gx + ex + n_gx, n_gx), lax.rem(gy + ey + n_gy, n_gy))
                 sides.append(((ex, ey), who))
-    everyone = z_peers + [who for _, who in plane] + [who for _, who in sides]
+    grp_peers = [who for (i, j, k), who in plane if j == 0 and k == 0]
+    near_z = [z_peers[i - 1] for i in range(1, n_z) if min(i, n_z - i) <= 2]
+    near = own_plane + grp_peers + near_z + [who for _, who in sides]
     barrier = pltpu.get_barrier_semaphore()
-    for who in everyone:
+    for who in near:
         pl.semaphore_signal(barrier, inc=1, device_id=who, device_id_type=MESH)
 
     def remote(src, dst, send, recv, who):
@@ -135,13 +144,29 @@
     def wait_bytes(ref, sem):
         pltpu.make_async_copy(ref, ref, sem).wait()
 
+    pairs = (
+        (ids_hbm, ids_ref),
+        (source_hbm, source_ref),
+        (diagonal_hbm, diagonal_ref),
+        (inverse_hbm, inverse_ref),
+        (xi_hbm, xi_ref),
+        (omega_hbm, omega_ref),
+        (psi_hbm, rows_k.at[pl.ds(0, k_psi * per_k)]),
+        (phi_hbm, rows_k.at[pl.ds(k_psi * per_k, k_phi * per_k)]),
+        (range_hbm, range_in),
+        (core_hbm, core_ref),
+    )
     loads = [
-        pltpu.make_async_copy(psi_hbm, rows_k.at[pl.ds(0, k_psi * per_k)], local_sem.at[0]),
-        pltpu.make_async_copy(phi_hbm, rows_k.at[pl.ds(k_psi * per_k, k_phi * per_k)], local_sem.at[1]),
-        pltpu.make_async_copy(range_hbm, range_in, local_sem.at[2]),
+        pltpu.make_async_copy(src, dst, local_sem.at[n]) for n, (src, dst) in enumerate(pairs)
     ]
     for load in loads:
         load.start()
+
+    def take_loads(count):
+        for _ in range(count):
+            loads.pop(0).wait()
+
+    take_loads(1)
 
     tile = (rows_y, LANES)
     sub = iota(tile, 0)
@@ -179,33 +204,36 @@
     def same(rank):
         return lambda cell: jnp.where(rank == cell, 1.0, 0.0)
 
+    plane_at = low_at * n_gy + gy
+    n_plane = n_low * n_gy
+
     def start_sum(which, halves):
         for i in range(2):
             sum_send[which, 0, pl.ds(i, 1), :] = halves[i]
-        zsum[which, z_at] = sum_send[which, 0]
+        psum[which, plane_at] = sum_send[which, 0]
+        for who in own_plane:
+            remote(sum_send.at[which, 0], psum.at[which, plane_at],
+                   sum_send_sem.at[which, 0], sum_recv_sem.at[which, 0], who)
+
+    def middle_sum(which):
+        wait_bytes(psum.at[which, pl.ds(0, n_plane - 1)], sum_recv_sem.at[which, 0])
+        total = psum[which, 0]
+        for i in range(1, n_plane):
+            total = total + psum[which, i]
+        sum_send[which, 1] = total
+        zsum[which, z_at] = sum_send[which, 1]
         for who in z_peers:
-            remote(sum_send.at[which, 0], zsum.at[which, z_at],
-                   sum_send_sem.at[which, 0], sum_recv_sem.at[which, 0], who)
-
-    def middle_sum(which):
-        wait_bytes(zsum.at[which, pl.ds(0, n_z - 1)], sum_recv_sem.at[which, 0])
+            remote(sum_send.at[which, 1], zsum.at[which, z_at],
+                   sum_send_sem.at[which, 1], sum_recv_sem.at[which, 1], who)
+
+    def end_sum(which):
+        wait_bytes(zsum.at[which, pl.ds(0, n_z - 1)], sum_recv_sem.at[which, 1])
         total = zsum[which, 0]
         for i in range(1, n_z):
             total = total + zsum[which, i]
-        sum_send[which, 1] = total
-        at = low_at * n_gy + gy
-        psum[which, at] = sum_send[which, 1]
-        for who in own_plane:
-            remote(sum_send.at[which, 1], psum.at[which, at],
-                   sum_send_sem.at[which, 1], sum_recv_sem.at[which, 1], who)
-
-    def end_sum(which):
-        n = n_low * n_gy
-        wait_bytes(psum.at[which, pl.ds(0, n - 1)], sum_recv_sem.at[which, 1])
-        total = psum[which, 0]
-        for i in range(1, n):
-            total = total + psum[which, i]
         return total * (coarse / total_cells)
+
+    take_loads(1)
 
     values = along_z(source_ref[...].reshape(per_k, cells_z))
     first_terms = [
@@ -213,9 +241,10 @@
     ]
     halves = to_boxes(first_terms)
 
-    pl.semaphore_wait(barrier, len(everyone))
+    pl.semaphore_wait(barrier, len(near))
     start_sum(0, halves)
 
+    take_loads(4)
     halo_copies = []
     y_from = {-1: pl.ds(0, HALO), 0: pl.ds(0, rows_y), 1: pl.ds(rows_y - HALO, HALO)}
     y_to = {-1: pl.ds(rows_y, HALO), 0: pl.ds(0, rows_y), 1: pl.ds(rows_y + HALO, HALO)}
@@ -248,6 +277,15 @@
     send_sides(source_ref, ext_s, HALO - 1, 8)
     ext_d[pl.ds(HALO, rows_x), pl.ds(0, rows_y), :] = diagonal_ref[...]
     ext_s[pl.ds(HALO, rows_x), pl.ds(0, rows_y), :] = source_ref[...]
+
+    reach, level = 2, 0
+    while reach < n_z // 2:
+        for i in (reach, n_z - reach):
+            pl.semaphore_signal(
+                chain.at[level], inc=1, device_id=z_peers[i - 1], device_id_type=MESH
+            )
+        pl.semaphore_wait(chain.at[level], 2)
+        reach, level = 2 * reach, level + 1
 
     middle_sum(0)
 
@@ -385,8 +423,7 @@
     pressure_copies = len(halo_copies)
     send_sides(ext_p.at[pl.ds(HALO, rows_x), pl.ds(0, rows_y), :], ext_p, HALO, 16)
 
-    for load in loads[:2]:
-        load.wait()
+    take_loads(2)
 
     def pack(at, carry):
         for kt in range(k_all // 8):
@@ -448,11 +485,12 @@
         out_send[0, pl.ds(i, 1), :] = sums[:, i * LANES : (i + 1) * LANES]
     for i in range(n_out // LANES, 4):
         out_send[0, pl.ds(i, 1), :] = jnp.zeros((1, LANES), f32)
-    zout[z_at] = out_send[0]
-    for who in z_peers:
-        remote(out_send.at[0], zout.at[z_at], sum_send_sem.at[2, 0], sum_recv_sem.at[2, 0], who)
-
-    loads[2].wait()
+    all_at = grp * n_plane + plane_at
+    pout[all_at] = out_send[0]
+    for _, who in plane:
+        remote(out_send.at[0], pout.at[all_at], sum_send_sem.at[2, 0], sum_recv_sem.at[2, 0], who)
+
+    take_loads(2)
 
     def add_range(k, carry):
         total = range_in[k]
@@ -462,51 +500,56 @@
         return carry
 
     lax.fori_loop(0, range_in.shape[0], add_range, 0)
-    store = pltpu.make_async_copy(range_done, range_out, local_sem.at[3])
-    store.start()
-
-    wait_bytes(zout.at[pl.ds(0, n_z - 1)], sum_recv_sem.at[2, 0])
+
+    n_all = n_grp * n_plane
+    wait_bytes(pout.at[pl.ds(0, n_all - 1)], sum_recv_sem.at[2, 0])
+    total = pout[0]
+    for i in range(1, n_all):
+        total = total + pout[i]
+    out_send[1] = total
+    zout[z_at] = out_send[1]
+    for who in z_peers:
+        remote(out_send.at[1], zout.at[z_at], sum_send_sem.at[2, 1], sum_recv_sem.at[2, 1], who)
+
+    n_core = xi_ref.shape[1]
+    by_t = iota((n_out, n_core), 0) // k_all
+    right = jnp.zeros((n_out, n_core), f32)
+    for t in range(n_grp):
+        line = jnp.broadcast_to(xi_ref[pl.ds(t, 1), :], (n_out, n_core))
+        right = jnp.where(by_t == t, line, right)
+    core_pick = iota((k_phi, n_out), 1) % k_all == iota((k_phi, n_out), 0) + k_psi
+    t_pick = iota((8, n_out), 1) // k_all == iota((8, n_out), 0)
+    row_pick = iota((n_out, k_psi), 0) % k_all == iota((n_out, k_psi), 1)
+    row_pick = jnp.where(row_pick, 1.0, 0.0)
+
+    wait_bytes(zout.at[pl.ds(0, n_z - 1)], sum_recv_sem.at[2, 1])
     total = zout[0]
     for i in range(1, n_z):
         total = total + zout[i]
-    out_send[1] = total
-    at = (grp * n_low + low_at) * n_gy + gy
-    pout[at] = out_send[1]
-    for _, who in plane:
-        remote(out_send.at[1], pout.at[at], sum_send_sem.at[2, 1], sum_recv_sem.at[2, 1], who)
-
-    n_core = core_ref.shape[0]
-    which_t = iota((n_out, LANES), 0) // k_all
-    right = jnp.where(which_t == iota((n_out, LANES), 1) - n_core, 1.0, 0.0)
-    lane_t = iota((n_out, 8), 1)
-    pick = jnp.where(iota((n_out, 8), 0) // k_all == lane_t, 1.0, 0.0)
-    xi = jnp.concatenate([xi_ref[...], jnp.zeros((n_core, 8 - n_grp), f32)], axis=1)
-    xi = jnp.concatenate([xi, jnp.zeros((LANES - n_core, 8), f32)], axis=0)
-    right = right + dot(pick, xi, NT, HIGHEST)
-    left_row = iota((k_all, n_out), 0)
-    left_pick = iota((k_all, n_out), 1) % k_all == left_row
-
-    n_plane = n_grp * n_low * n_gy
-    wait_bytes(pout.at[pl.ds(0, n_plane - 1)], sum_recv_sem.at[2, 1])
-    total = pout[0]
-    for i in range(1, n_plane):
-        total = total + pout[i]
     line = jnp.concatenate([total[i : i + 1] for i in range(n_out // LANES)], axis=1)
-    left = jnp.where(left_pick, jnp.broadcast_to(line, (k_all, n_out)), 0.0)
-    result = dot(left, right, NN, HIGHEST)
-    corange_out[...] = result[:k_psi, n_core : n_core + n_grp]
-    core_out[...] = core_ref[...] + result[k_psi:, :n_core]
-
-    store.wait()
+    left = jnp.where(core_pick, jnp.broadcast_to(line, (k_phi, n_out)), 0.0)
+    core_out[...] = core_ref[...] + dot(left, right, NN, HIGHEST)
+    left = jnp.where(t_pick, jnp.broadcast_to(line, (8, n_out)), 0.0)
+    corange_out[...] = dot(left, row_pick, NN, HIGHEST)[:n_grp]
+
     for copy in halo_copies:
         copy.wait_send()
     for copy in snap_copies:
         copy.wait_send()
     for which in range(2):
-        wait_bytes(zsum.at[which, pl.ds(0, n_z - 1)], sum_send_sem.at[which, 0])
-        wait_bytes(psum.at[which, pl.ds(0, n_low * n_gy - 1)], sum_send_sem.at[which, 1])
-    wait_bytes(zout.at[pl.ds(0, n_z - 1)], sum_send_sem.at[2, 0])
-    wait_bytes(pout.at[pl.ds(0, n_plane - 1)], sum_send_sem.at[2, 1])
+        wait_bytes(psum.at[which, pl.ds(0, n_plane - 1)], sum_send_sem.at[which, 0])
+        wait_bytes(zsum.at[which, pl.ds(0, n_z - 1)], sum_send_sem.at[which, 1])
+    wait_bytes(pout.at[pl.ds(0, n_all - 1)], sum_send_sem.at[2, 0])
+    wait_bytes(zout.at[pl.ds(0, n_z - 1)], sum_send_sem.at[2, 1])
+
+
+def finish(range_in, corange_in, core_in, range_out, corange_out, core_out, sems):
+    pairs = ((range_in, range_out), (corange_in, corange_out), (core_in, core_out))
+    stores = [pltpu.make_async_copy(src, dst, sems.at[n]) for n, (src, dst) in enumerate(pairs)]
+    for store in stores:
+        store.start()
+    for store in stores:
+        store.wait()
 
 
 def solution(mesh):
@@ -535,21 +578,26 @@
         per_k = rows_x * rows_y
         coarse = coarse_inverse.shape[0]
         vmem = pl.BlockSpec(memory_space=pltpu.VMEM)
-        smem = pl.BlockSpec(memory_space=pltpu.SMEM)
         hbm = pl.BlockSpec(memory_space=pl.ANY)
         ext = pltpu.VMEM((n_ext, 2 * rows_y, cells_z), f32)
         call = pl.pallas_call(
             functools.partial(kernel, (n_grp, n_gx, n_gy, n_z, total_cells)),
             out_shape=(
-                jax.ShapeDtypeStruct((k_range, per_k, LANES), f32),
-                jax.ShapeDtypeStruct((k_psi, n_grp), f32),
-                jax.ShapeDtypeStruct(core_sketch.shape, f32),
+                pltpu.VMEM((k_range, per_k, LANES), f32),
+                pltpu.VMEM((n_grp, k_psi), f32),
+                pltpu.VMEM(core_sketch.shape, f32),
             ),
-            in_specs=[vmem, vmem, vmem, vmem, smem, hbm, hbm, vmem, hbm, vmem],
-            out_specs=(hbm, vmem, vmem),
+            in_specs=[hbm] * 10,
+            out_specs=(vmem, vmem, vmem),
             scratch_shapes=[
+                pltpu.VMEM((rows_x, rows_y, cells_z), f32),
+                pltpu.VMEM((rows_x, rows_y, cells_z), f32),
+                pltpu.VMEM((rows_x, rows_y, cells_z), jnp.int32),
+                pltpu.VMEM(coarse_inverse.shape, f32),
+                pltpu.SMEM(omega_rows.shape, f32),
+                pltpu.VMEM((n_grp, xi_cols.shape[0]), f32),
+                pltpu.VMEM(core_sketch.shape, f32),
                 pltpu.VMEM((k_all * per_k, LANES), f32),
-                pltpu.VMEM((k_range, per_k, LANES), f32),
                 pltpu.VMEM((k_range, per_k, LANES), f32),
                 ext,
                 ext,
@@ -572,13 +620,14 @@
                 pltpu.VMEM((2, 4, LANES), f32),
                 pltpu.VMEM((n_z, 4, LANES), f32),
                 pltpu.VMEM((n_grp * n_low * n_gy, 4, LANES), f32),
-                pltpu.SemaphoreType.DMA((4,)),
+                pltpu.SemaphoreType.DMA((10,)),
                 pltpu.SemaphoreType.DMA((28,)),
                 pltpu.SemaphoreType.DMA((28,)),
                 pltpu.SemaphoreType.DMA((3, 2)),
                 pltpu.SemaphoreType.DMA((3, 2)),
                 pltpu.SemaphoreType.DMA((n_grp - 1,)),
                 pltpu.SemaphoreType.DMA((1,)),
+                pltpu.SemaphoreType.REGULAR((2,)),
             ],
             compiler_params=pltpu.CompilerParams(
                 collective_id=0, has_side_effects=True
@@ -593,11 +642,24 @@
             omega_rows,
             psi.reshape(k_psi * per_k, LANES),
             phi.reshape(k_phi * per_k, LANES),
-            xi_cols,
+            xi_cols.T,
             range_sketch.reshape(k_range, per_k, LANES),
             core_sketch,
         )
-        return range_new.reshape(range_sketch.shape), corange_cols, core_new
+        range_new, corange_cols, core_new = pl.pallas_call(
+            finish,
+            out_shape=(
+                jax.ShapeDtypeStruct((k_range, per_k, LANES), f32),
+                jax.ShapeDtypeStruct((n_grp, k_psi), f32),
+                jax.ShapeDtypeStruct(core_sketch.shape, f32),
+            ),
+            in_specs=[vmem] * 3,
+            out_specs=(hbm, hbm, hbm),
+            scratch_shapes=[pltpu.SemaphoreType.DMA((3,))],
+            compiler_params=pltpu.CompilerParams(vmem_limit_bytes=1 << 21),
+            name="finish",
+        )(range_new, corange_cols, core_new)
+        return range_new.reshape(range_sketch.shape), corange_cols.T, core_new
 
     return jax.shard_map(
         body,

time: 66.4 us -> 59.2 us (0.89)
  local copies, waits for them, and re-layouts: 5.25 us -> 0 us
  Pallas kernels: 60.3 us -> 58.4 us
    unnamed x8 -> x0, local copies, waits for them, and re-layouts: 5.25 us -> none
    pallas_call x1, Pallas kernels: 60.3 us -> 57.6 us  [body(): call(sources[0], diagonal, coarse_ids, coarse_inverse, omega_rows, psi.re...]
    pallas_call x0 -> x1, Pallas kernels: none -> 0.83 us  [body(): pl.pallas_call(finish, out_shape=(jax.ShapeDtypeStruct((k_range, per_k, L...]
where the time goes in v2:
time: 59.2 us; the launch traced here: 59 us
  Pallas kernels  58.4 us (99%)
  between operations  0.64 us (1%)
    pallas_call x1, Pallas kernels, body(): call(sources[0], diagonal, coarse_ids, coarse_inverse, omega_rows, psi.re...  57.6 us

profile of v2, /device:TPU:1, one launch (start us, length us, event | category | flops | bytes accessed | tf_op | source)
XLA Modules:
  0.0 59.0 jit_solution(4422315854157910203)
XLA Ops:
  0.6 57.6 %two_level_sketch.1 = (f32[32,32,128]{2,1,0:T(8,128)S(1)}, f32[4,32]{1,0:T(4,128)S(1)}, f32[64,64]{1,0:T(8,128)S(1)}) custom-call(f32[4,8,512]{2,1,0:T(8,128)} %bitcast.10, f32[4,8,512]{2,1,0:T(8,128)} %diagonal_hbm.1, s32[4,8,512]{2,1,0:T(8,128)} %ids_hbm.1, f32[256,256]{1,0:T(8,128)} %inverse_hbm.1, f32[4,32]{1,0:T(4,128)} %omega_hbm.1, ...), custom_call_target="tpu_custom_call" | custom-call | tf_op jit(solution)/shard_map/two_level_sketch/pallas_call | solution.py:637
  58.2 0.8 %finish.1 = (f32[32,32,128]{2,1,0:T(8,128)}, f32[4,32]{1,0:T(4,128)}, f32[64,64]{1,0:T(8,128)}) custom-call(f32[32,32,128]{2,1,0:T(8,128)S(1)} %get-tuple-element.9.range_in, f32[4,32]{1,0:T(4,128)S(1)} %get-tuple-element.10.corange_in, f32[64,64]{1,0:T(8,128)S(1)} %get-tuple-element.11.core_in), custom_call_target="tpu_custom_call" | custom-call | tf_op jit(solution)/shard_map/finish/pallas_call | solution.py:649

commit v3 on v2

--- a/solution.py
+++ b/solution.py
@@ -93,6 +93,7 @@
     snap_send,
     snap_recv,
     chain,
+    inverse_parts,
 ):
     n_grp, n_gx, n_gy, n_z, total_cells = sizes
     n_low = n_gx // n_z
@@ -119,7 +120,11 @@
                         lax.rem(gy + k, n_gy),
                     )
                     plane.append(((i, j, k), who))
+    plane.sort(key=lambda peer: -(min(peer[0][0], n_grp - peer[0][0]) + peer[0][1]
+                                  + min(peer[0][2], n_gy - peer[0][2])))
     own_plane = [who for (i, j, k), who in plane if i == 0]
+    z_order = sorted(range(n_z - 1), key=lambda i: -min(i + 1, n_z - 1 - i))
+    far_first = [z_peers[i] for i in z_order]
     sides = []
     for ex in (-1, 0, 1):
         for ey in (-1, 0, 1):
@@ -129,21 +134,6 @@
     grp_peers = [who for (i, j, k), who in plane if j == 0 and k == 0]
     near_z = [z_peers[i - 1] for i in range(1, n_z) if min(i, n_z - i) <= 2]
     near = own_plane + grp_peers + near_z + [who for _, who in sides]
-    barrier = pltpu.get_barrier_semaphore()
-    for who in near:
-        pl.semaphore_signal(barrier, inc=1, device_id=who, device_id_type=MESH)
-
-    def remote(src, dst, send, recv, who):
-        copy = pltpu.make_async_remote_copy(
-            src_ref=src, dst_ref=dst, send_sem=send, recv_sem=recv,
-            device_id=who, device_id_type=MESH,
-        )
-        copy.start()
-        return copy
-
-    def wait_bytes(ref, sem):
-        pltpu.make_async_copy(ref, ref, sem).wait()
-
     pairs = (
         (ids_hbm, ids_ref),
         (source_hbm, source_ref),
@@ -159,8 +149,26 @@
     loads = [
         pltpu.make_async_copy(src, dst, local_sem.at[n]) for n, (src, dst) in enumerate(pairs)
     ]
-    for load in loads:
+    for load in loads[:2]:
         load.start()
+    barrier = pltpu.get_barrier_semaphore()
+    for who in near:
+        pl.semaphore_signal(barrier, inc=1, device_id=who, device_id_type=MESH)
+    for load in loads[2:]:
+        load.start()
+
+    def remote(src, dst, send, recv, who):
+        copy = pltpu.make_async_remote_copy(
+            src_ref=src, dst_ref=dst, send_sem=send, recv_sem=recv,
+            device_id=who, device_id_type=MESH,
+        )
+        copy.start()
+        return copy
+
+    ends = []
+
+    def wait_bytes(ref, sem):
+        pltpu.make_async_copy(ref, ref, sem).wait()
 
     def take_loads(count):
         for _ in range(count):
@@ -214,6 +222,7 @@
         for who in own_plane:
             remote(sum_send.at[which, 0], psum.at[which, plane_at],
                    sum_send_sem.at[which, 0], sum_recv_sem.at[which, 0], who)
+        ends.append(lambda: wait_bytes(psum.at[which, pl.ds(0, n_plane - 1)], sum_send_sem.at[which, 0]))
 
     def middle_sum(which):
         wait_bytes(psum.at[which, pl.ds(0, n_plane - 1)], sum_recv_sem.at[which, 0])
@@ -222,9 +231,10 @@
             total = total + psum[which, i]
         sum_send[which, 1] = total
         zsum[which, z_at] = sum_send[which, 1]
-        for who in z_peers:
+        for who in far_first:
             remote(sum_send.at[which, 1], zsum.at[which, z_at],
                    sum_send_sem.at[which, 1], sum_recv_sem.at[which, 1], who)
+        ends.append(lambda: wait_bytes(zsum.at[which, pl.ds(0, n_z - 1)], sum_send_sem.at[which, 1]))
 
     def end_sum(which):
         wait_bytes(zsum.at[which, pl.ds(0, n_z - 1)], sum_recv_sem.at[which, 1])
@@ -242,9 +252,20 @@
     halves = to_boxes(first_terms)
 
     pl.semaphore_wait(barrier, len(near))
+    reaches = []
+    while 2 << len(reaches) < n_z // 2:
+        reaches.append(2 << len(reaches))
+
+    def greet(level):
+        for i in (reaches[level], n_z - reaches[level]):
+            pl.semaphore_signal(
+                chain.at[level], inc=1, device_id=z_peers[i - 1], device_id_type=MESH
+            )
+
+    if reaches:
+        greet(0)
     start_sum(0, halves)
-
-    take_loads(4)
+    take_loads(1)
     halo_copies = []
     y_from = {-1: pl.ds(0, HALO), 0: pl.ds(0, rows_y), 1: pl.ds(rows_y - HALO, HALO)}
     y_to = {-1: pl.ds(rows_y, HALO), 0: pl.ds(0, rows_y), 1: pl.ds(rows_y + HALO, HALO)}
@@ -256,15 +277,25 @@
             return rows_x - depth, HALO - depth, depth
         return 0, HALO + rows_x, depth
 
-    def send_sides(src, ext, depth, base):
+    def send_sides(src, ext, depth, base, first_phase):
         for n, ((ex, ey), who) in enumerate(sides):
+            if (ey == 0) != first_phase:
+                continue
             first, to, count = x_rows(ex, depth - (1 if ex and ey else 0))
             halo_copies.append(
                 remote(src.at[pl.ds(first, count), y_from[ey], :],
                        ext.at[pl.ds(to, count), y_to[ey], :],
                        halo_send.at[base + n], halo_recv.at[base + n], who)
             )
-
+            ends.append(halo_copies[-1].wait_send)
+
+    send_sides(diagonal_ref, ext_d, HALO - 1, 0, True)
+    send_sides(source_ref, ext_s, HALO - 1, 8, True)
+    for level in range(len(reaches)):
+        pl.semaphore_wait(chain.at[level], 2)
+        if level + 1 < len(reaches):
+            greet(level + 1)
+    middle_sum(0)
     n_rank = 0
     for (ex, ey), who in sides:
         if not (ex and ey):
@@ -272,22 +303,23 @@
                 remote(ranks, ranks_in.at[n_rank],
                        halo_send.at[24 + n_rank], halo_recv.at[24 + n_rank], who)
             )
+            ends.append(halo_copies[-1].wait_send)
             n_rank += 1
-    send_sides(diagonal_ref, ext_d, HALO - 1, 0)
-    send_sides(source_ref, ext_s, HALO - 1, 8)
+    send_sides(diagonal_ref, ext_d, HALO - 1, 0, False)
+    send_sides(source_ref, ext_s, HALO - 1, 8, False)
     ext_d[pl.ds(HALO, rows_x), pl.ds(0, rows_y), :] = diagonal_ref[...]
     ext_s[pl.ds(HALO, rows_x), pl.ds(0, rows_y), :] = source_ref[...]
 
-    reach, level = 2, 0
-    while reach < n_z // 2:
-        for i in (reach, n_z - reach):
-            pl.semaphore_signal(
-                chain.at[level], inc=1, device_id=z_peers[i - 1], device_id_type=MESH
-            )
-        pl.semaphore_wait(chain.at[level], 2)
-        reach, level = 2 * reach, level + 1
-
-    middle_sum(0)
+    take_loads(5)
+    for n, part in enumerate(split3(inverse_ref[...])):
+        inverse_parts[n] = part
+
+    def pack(at, carry):
+        for kt in range(k_all // 8):
+            packed[kt, at] = rows_k[pl.ds(kt * 8 * per_k + at, 8, stride=per_k), :]
+        return carry
+
+    lax.fori_loop(0, per_k, pack, 0)
 
     for copy in halo_copies:
         copy.wait_recv()
@@ -345,17 +377,22 @@
         after = jnp.where(z_lane == cells_z - 1, 0.0, pltpu.roll(values, cells_z - 1, 1))
         return before + after
 
-    def correct(which, store):
-        rhs = end_sum(which)
-        top = jnp.broadcast_to(rhs[0:1], (8, LANES))
-        bottom = jnp.broadcast_to(rhs[1:2], (8, LANES))
-        solved = dot(top, inverse_ref[:, 0:LANES], NT, HIGHEST)
-        solved = solved + dot(bottom, inverse_ref[:, LANES:], NT, HIGHEST)
+    def correct(rhs, store):
+        line = jnp.concatenate([rhs[0:1], rhs[1:2]], axis=1)
+        at = iota((8, coarse), 0)
+        left = jnp.zeros((8, coarse), f32)
+        for n, part in enumerate(split3(line)):
+            left = jnp.where(at == n, part.astype(f32), left)
+        left = left.astype(bf16)
+        solved = dot(left, inverse_parts[0], NT)
+        solved = solved + jnp.where(at < 2, dot(left, inverse_parts[1], NT), 0.0)
+        solved = solved + jnp.where(at < 1, dot(left, inverse_parts[2], NT), 0.0)
+        solved = jnp.sum(solved, axis=0, keepdims=True)
         pairs = XY_CUTS * XY_CUTS
         row = iota((pairs, coarse), 0)
         column = iota((pairs, coarse), 1)
         spread = jnp.where(
-            column // Z_CUTS == row, jnp.broadcast_to(solved[0:1], (pairs, coarse)), 0.0
+            column // Z_CUTS == row, jnp.broadcast_to(solved, (pairs, coarse)), 0.0
         )
         parts = dot(jnp.concatenate(split3(spread), axis=0), map_g[...], NN)
         boxes = parts[:pairs] + parts[pairs : 2 * pairs] + parts[2 * pairs :]
@@ -402,7 +439,8 @@
     def store_first(r, picked):
         field_a[r] = picked
 
-    correct(0, store_first)
+    rhs = end_sum(0)
+    correct(rhs, store_first)
 
     def last_first(r, old):
         ext_p[r, pl.ds(0, rows_y), :] = last_value(r, old)
@@ -419,19 +457,14 @@
     for x in range(2 * rows_x):
         count = same(box[x]) if x < rows_x else beside(x - rows_x)
         terms.append((values[x * rows_y : (x + 1) * rows_y], count))
-    start_sum(1, to_boxes(terms))
+    halves = to_boxes(terms)
+    start_sum(1, halves)
     pressure_copies = len(halo_copies)
-    send_sides(ext_p.at[pl.ds(HALO, rows_x), pl.ds(0, rows_y), :], ext_p, HALO, 16)
-
-    take_loads(2)
-
-    def pack(at, carry):
-        for kt in range(k_all // 8):
-            packed[kt, at] = rows_k[pl.ds(kt * 8 * per_k + at, 8, stride=per_k), :]
-        return carry
-
-    lax.fori_loop(0, per_k, pack, 0)
+    own_p = ext_p.at[pl.ds(HALO, rows_x), pl.ds(0, rows_y), :]
+    send_sides(own_p, ext_p, HALO, 16, True)
+
     middle_sum(1)
+    send_sides(own_p, ext_p, HALO, 16, False)
     for copy in halo_copies[pressure_copies:]:
         copy.wait_recv()
 
@@ -439,47 +472,55 @@
         here = (rank_x_wide[r] >= 0.0) & (rank_y_wide >= 0.0)
         field_a[r] = picked + jnp.where(here, ext_p[r], 0.0)
 
-    correct(1, store_second)
+    rhs = end_sum(1)
+    correct(rhs, store_second)
 
     def last_second(r, old):
         final[pl.ds((r - HALO) * rows_y, rows_y), :] = last_value(r, old)
 
     smooth(last_second)
 
-    snap_copies = []
+    n_far = n_grp // 2
     own_cells = pl.ds(pl.multiple_of(grp * per_k, per_k), per_k)
-    for i in range(1, n_grp):
-        other = lax.rem(grp + i, n_grp)
+    pair_at = lax.div(grp, n_far) * n_far
+    far_at = n_far - pair_at
+    core_at = grp - pair_at
+    others = [(0, far_at + lax.rem(core_at + i, n_far)) for i in range(n_far)]
+    others += [(1, pair_at + lax.rem(core_at + i, n_far)) for i in range(1, n_far)]
+    for n, (near_by, other) in enumerate(others):
         lanes = pl.ds(pl.multiple_of(other * LANES, LANES), LANES)
-        snap_copies.append(
-            remote(final.at[:, lanes], snap.at[own_cells],
-                   snap_send.at[i - 1], snap_recv.at[0], (other, gx, gy))
-        )
+        copy = remote(final.at[:, lanes], snap.at[own_cells],
+                      snap_send.at[n], snap_recv.at[near_by], (other, gx, gy))
+        ends.append(copy.wait_send)
     own_lanes = pl.ds(pl.multiple_of(grp * LANES, LANES), LANES)
     snap[own_cells, :] = final[:, own_lanes]
-    wait_bytes(snap.at[pl.ds(0, (n_grp - 1) * per_k)], snap_recv.at[0])
-
-    group = 6
-    for base in range(0, k_all // 8, group):
-
+
+    def products(base):
         def step(at, carry):
             rows = [
-                jnp.broadcast_to(snap[pl.ds(t * per_k + at, 1), :], (8, LANES))
-                for t in range(n_grp)
+                jnp.broadcast_to(snap[pl.ds((base + t) * per_k + at, 1), :], (8, LANES))
+                for t in range(n_far)
             ]
             out = []
-            for n in range(group):
-                taken = packed[base + n, at]
-                for t in range(n_grp):
-                    out.append(carry[n * n_grp + t] + taken * rows[t])
+            for kt in range(k_all // 8):
+                taken = packed[kt, at]
+                for t in range(n_far):
+                    out.append(carry[kt * n_far + t] + taken * rows[t])
             return tuple(out)
 
-        zeros = tuple(jnp.zeros((8, LANES), f32) for _ in range(group * n_grp))
+        zeros = tuple(jnp.zeros((8, LANES), f32) for _ in range(k_all // 8 * n_far))
         sums = lax.fori_loop(0, per_k, step, zeros)
-        for n in range(group):
-            for t in range(n_grp):
-                reduced[pl.ds(t * k_all + (base + n) * 8, 8), :] = sums[n * n_grp + t]
-    sums = dot(jnp.ones((8, LANES), f32), reduced[...], NT, HIGHEST)[0:1]
+        for kt in range(k_all // 8):
+            for t in range(n_far):
+                to = pl.multiple_of((base + t) * k_all, 8) + kt * 8
+                reduced[pl.ds(to, 8), :] = sums[kt * n_far + t]
+
+    wait_bytes(snap.at[pl.ds(0, (n_far - 1) * per_k)], snap_recv.at[1])
+    products(pair_at)
+    wait_bytes(snap.at[pl.ds(0, n_far * per_k)], snap_recv.at[0])
+    products(far_at)
+    ones = jnp.ones((16, LANES), bf16)
+    sums = sum(dot(ones, part, NT)[0:1] for part in split3(reduced[...]))
     n_out = n_grp * k_all
     for i in range(n_out // LANES):
         out_send[0, pl.ds(i, 1), :] = sums[:, i * LANES : (i + 1) * LANES]
@@ -489,6 +530,8 @@
     pout[all_at] = out_send[0]
     for _, who in plane:
         remote(out_send.at[0], pout.at[all_at], sum_send_sem.at[2, 0], sum_recv_sem.at[2, 0], who)
+    n_all = n_grp * n_plane
+    ends.append(lambda: wait_bytes(pout.at[pl.ds(0, n_all - 1)], sum_send_sem.at[2, 0]))
 
     take_loads(2)
 
@@ -501,46 +544,51 @@
 
     lax.fori_loop(0, range_in.shape[0], add_range, 0)
 
-    n_all = n_grp * n_plane
     wait_bytes(pout.at[pl.ds(0, n_all - 1)], sum_recv_sem.at[2, 0])
     total = pout[0]
     for i in range(1, n_all):
         total = total + pout[i]
     out_send[1] = total
     zout[z_at] = out_send[1]
-    for who in z_peers:
+    for who in far_first:
         remote(out_send.at[1], zout.at[z_at], sum_send_sem.at[2, 1], sum_recv_sem.at[2, 1], who)
 
     n_core = xi_ref.shape[1]
     by_t = iota((n_out, n_core), 0) // k_all
-    right = jnp.zeros((n_out, n_core), f32)
+    columns = jnp.zeros((n_out, n_core), f32)
     for t in range(n_grp):
         line = jnp.broadcast_to(xi_ref[pl.ds(t, 1), :], (n_out, n_core))
-        right = jnp.where(by_t == t, line, right)
+        columns = jnp.where(by_t == t, line, columns)
+    row_pick = iota((n_out, n_core), 0) % k_all == iota((n_out, n_core), 1)
+    right = [part.astype(f32) for part in split3(columns)]
+    right.append(jnp.where(row_pick, 1.0, 0.0))
+    right = jnp.concatenate(right, axis=1).astype(bf16)
     core_pick = iota((k_phi, n_out), 1) % k_all == iota((k_phi, n_out), 0) + k_psi
-    t_pick = iota((8, n_out), 1) // k_all == iota((8, n_out), 0)
-    row_pick = iota((n_out, k_psi), 0) % k_all == iota((n_out, k_psi), 1)
-    row_pick = jnp.where(row_pick, 1.0, 0.0)
+    t_pick = iota((16, n_out), 1) // k_all == iota((16, n_out), 0)
+    for end in ends:
+        end()
+    ends = [lambda: wait_bytes(zout.at[pl.ds(0, n_z - 1)], sum_send_sem.at[2, 1])]
 
     wait_bytes(zout.at[pl.ds(0, n_z - 1)], sum_recv_sem.at[2, 1])
     total = zout[0]
     for i in range(1, n_z):
         total = total + zout[i]
     line = jnp.concatenate([total[i : i + 1] for i in range(n_out // LANES)], axis=1)
-    left = jnp.where(core_pick, jnp.broadcast_to(line, (k_phi, n_out)), 0.0)
-    core_out[...] = core_ref[...] + dot(left, right, NN, HIGHEST)
-    left = jnp.where(t_pick, jnp.broadcast_to(line, (8, n_out)), 0.0)
-    corange_out[...] = dot(left, row_pick, NN, HIGHEST)[:n_grp]
-
-    for copy in halo_copies:
-        copy.wait_send()
-    for copy in snap_copies:
-        copy.wait_send()
-    for which in range(2):
-        wait_bytes(psum.at[which, pl.ds(0, n_plane - 1)], sum_send_sem.at[which, 0])
-        wait_bytes(zsum.at[which, pl.ds(0, n_z - 1)], sum_send_sem.at[which, 1])
-    wait_bytes(pout.at[pl.ds(0, n_all - 1)], sum_send_sem.at[2, 0])
-    wait_bytes(zout.at[pl.ds(0, n_z - 1)], sum_send_sem.at[2, 1])
+    left = []
+    for part in split3(line):
+        part = part.astype(f32)
+        left.append(jnp.where(core_pick, jnp.broadcast_to(part, (k_phi, n_out)), 0.0))
+        left.append(jnp.where(t_pick, jnp.broadcast_to(part, (16, n_out)), 0.0))
+    parts = dot(jnp.concatenate(left, axis=0).astype(bf16), right, NN)
+    n = k_phi + 16
+    result = parts[:n] + parts[n : 2 * n] + parts[2 * n :]
+    images = result[:k_phi]
+    core_sum = images[:, :n_core] + images[:, n_core : 2 * n_core] + images[:, 2 * n_core : 3 * n_core]
+    core_out[...] = core_ref[...] + core_sum
+    corange_out[...] = result[k_phi : k_phi + n_grp, 3 * n_core : 3 * n_core + k_psi]
+
+    for end in ends:
+        end()
 
 
 def finish(range_in, corange_in, core_in, range_out, corange_out, core_out, sems):
@@ -626,8 +674,9 @@
                 pltpu.SemaphoreType.DMA((3, 2)),
                 pltpu.SemaphoreType.DMA((3, 2)),
                 pltpu.SemaphoreType.DMA((n_grp - 1,)),
-                pltpu.SemaphoreType.DMA((1,)),
+                pltpu.SemaphoreType.DMA((2,)),
                 pltpu.SemaphoreType.REGULAR((2,)),
+                pltpu.VMEM((3, coarse, coarse), bf16),
             ],
             compiler_params=pltpu.CompilerParams(
                 collective_id=0, has_side_effects=True

time: 59.2 us -> 57.1 us (0.965)
  Pallas kernels: 58.4 us -> 56.3 us
    pallas_call x1, Pallas kernels: 57.6 us -> 55.5 us  [body(): call(sources[0], diagonal, coarse_ids, coarse_inverse, omega_rows, psi.re...]
where the time goes in v3:
time: 57.1 us; the launch traced here: 57 us
  Pallas kernels  56.3 us (99%)
  between operations  0.64 us (1%)
    pallas_call x1, Pallas kernels, body(): call(sources[0], diagonal, coarse_ids, coarse_inverse, omega_rows, psi.re...  55.5 us

profile of v3, /device:TPU:1, one launch (start us, length us, event | category | flops | bytes accessed | tf_op | source)
XLA Modules:
  0.0 57.0 jit_solution(13227569153058684014)
XLA Ops:
  0.6 55.5 %two_level_sketch.1 = (f32[32,32,128]{2,1,0:T(8,128)S(1)}, f32[4,32]{1,0:T(4,128)S(1)}, f32[64,64]{1,0:T(8,128)S(1)}) custom-call(f32[4,8,512]{2,1,0:T(8,128)} %bitcast.10, f32[4,8,512]{2,1,0:T(8,128)} %diagonal_hbm.1, s32[4,8,512]{2,1,0:T(8,128)} %ids_hbm.1, f32[256,256]{1,0:T(8,128)} %inverse_hbm.1, f32[4,32]{1,0:T(4,128)} %omega_hbm.1, ...), custom_call_target="tpu_custom_call" | custom-call | tf_op jit(solution)/shard_map/two_level_sketch/pallas_call | solution.py:686
  56.1 0.8 %finish.1 = (f32[32,32,128]{2,1,0:T(8,128)}, f32[4,32]{1,0:T(4,128)}, f32[64,64]{1,0:T(8,128)}) custom-call(f32[32,32,128]{2,1,0:T(8,128)S(1)} %get-tuple-element.9.range_in, f32[4,32]{1,0:T(4,128)S(1)} %get-tuple-element.10.corange_in, f32[64,64]{1,0:T(8,128)S(1)} %get-tuple-element.11.core_in), custom_call_target="tpu_custom_call" | custom-call | tf_op jit(solution)/shard_map/finish/pallas_call | solution.py:698

commit v4 on v3

--- a/solution.py
+++ b/solution.py
@@ -94,6 +94,7 @@
     snap_recv,
     chain,
     inverse_parts,
+    pair_send,
 ):
     n_grp, n_gx, n_gy, n_z, total_cells = sizes
     n_low = n_gx // n_z
@@ -132,8 +133,8 @@
                 who = (grp, lax.rem(gx + ex + n_gx, n_gx), lax.rem(gy + ey + n_gy, n_gy))
                 sides.append(((ex, ey), who))
     grp_peers = [who for (i, j, k), who in plane if j == 0 and k == 0]
-    near_z = [z_peers[i - 1] for i in range(1, n_z) if min(i, n_z - i) <= 2]
-    near = own_plane + grp_peers + near_z + [who for _, who in sides]
+    near_z = [z_peers[i - 1] for i in range(1, n_z) if min(i, n_z - i) <= 3]
+    near = own_plane + near_z + [who for (_, ey), who in sides if ey == 0] + grp_peers
     pairs = (
         (ids_hbm, ids_ref),
         (source_hbm, source_ref),
@@ -252,9 +253,10 @@
     halves = to_boxes(first_terms)
 
     pl.semaphore_wait(barrier, len(near))
-    reaches = []
-    while 2 << len(reaches) < n_z // 2:
-        reaches.append(2 << len(reaches))
+    reaches, known = [], 3
+    while known < n_z // 2:
+        reaches.append(min(3, n_z // 2 - known))
+        known += reaches[-1]
 
     def greet(level):
         for i in (reaches[level], n_z - reaches[level]):
@@ -527,11 +529,30 @@
     for i in range(n_out // LANES, 4):
         out_send[0, pl.ds(i, 1), :] = jnp.zeros((1, LANES), f32)
     all_at = grp * n_plane + plane_at
+    summing = core_at == n_far - 1
+    partner = (grp + 1 - 2 * core_at, gx, gy)
+    pair_index = lax.div(grp, n_far)
+    chips = []
+    for i in range(n_grp // n_far):
+        for j in range(n_low):
+            for k in range(n_gy):
+                who = (
+                    lax.rem(pair_index + i, n_grp // n_far) * n_far + n_far - 1,
+                    lax.rem(gx + j * n_z, n_gx),
+                    lax.rem(gy + k, n_gy),
+                )
+                chips.append((2 * i + j + min(k, n_gy - k), who))
+    chips = [who for away, who in sorted(chips, key=lambda chip: -chip[0]) if away]
     pout[all_at] = out_send[0]
-    for _, who in plane:
+    for who in chips:
         remote(out_send.at[0], pout.at[all_at], sum_send_sem.at[2, 0], sum_recv_sem.at[2, 0], who)
+    ends.append(lambda: wait_bytes(pout.at[pl.ds(0, len(chips))], sum_send_sem.at[2, 0]))
+
+    @pl.when(jnp.logical_not(summing))
+    def _():
+        remote(out_send.at[0], pout.at[all_at], pair_send.at[0], sum_recv_sem.at[2, 0], partner)
+
     n_all = n_grp * n_plane
-    ends.append(lambda: wait_bytes(pout.at[pl.ds(0, n_all - 1)], sum_send_sem.at[2, 0]))
 
     take_loads(2)
 
@@ -544,14 +565,19 @@
 
     lax.fori_loop(0, range_in.shape[0], add_range, 0)
 
-    wait_bytes(pout.at[pl.ds(0, n_all - 1)], sum_recv_sem.at[2, 0])
-    total = pout[0]
-    for i in range(1, n_all):
-        total = total + pout[i]
-    out_send[1] = total
-    zout[z_at] = out_send[1]
-    for who in far_first:
-        remote(out_send.at[1], zout.at[z_at], sum_send_sem.at[2, 1], sum_recv_sem.at[2, 1], who)
+    @pl.when(summing)
+    def _():
+        wait_bytes(pout.at[pl.ds(0, n_all - 1)], sum_recv_sem.at[2, 0])
+        total = pout[0]
+        for i in range(1, n_all):
+            total = total + pout[i]
+        out_send[1] = total
+        zout[z_at] = out_send[1]
+        for _, who_x, who_y in far_first:
+            for who in ((partner[0], who_x, who_y), (grp, who_x, who_y)):
+                remote(out_send.at[1], zout.at[z_at],
+                       sum_send_sem.at[2, 1], sum_recv_sem.at[2, 1], who)
+        remote(out_send.at[1], zout.at[z_at], sum_send_sem.at[2, 1], sum_recv_sem.at[2, 1], partner)
 
     n_core = xi_ref.shape[1]
     by_t = iota((n_out, n_core), 0) // k_all
@@ -567,9 +593,15 @@
     t_pick = iota((16, n_out), 1) // k_all == iota((16, n_out), 0)
     for end in ends:
         end()
-    ends = [lambda: wait_bytes(zout.at[pl.ds(0, n_z - 1)], sum_send_sem.at[2, 1])]
-
-    wait_bytes(zout.at[pl.ds(0, n_z - 1)], sum_recv_sem.at[2, 1])
+
+    @pl.when(summing)
+    def _():
+        wait_bytes(zout.at[pl.ds(0, n_z - 1)], sum_recv_sem.at[2, 1])
+
+    @pl.when(jnp.logical_not(summing))
+    def _():
+        wait_bytes(zout, sum_recv_sem.at[2, 1])
+
     total = zout[0]
     for i in range(1, n_z):
         total = total + zout[i]
@@ -587,8 +619,13 @@
     core_out[...] = core_ref[...] + core_sum
     corange_out[...] = result[k_phi : k_phi + n_grp, 3 * n_core : 3 * n_core + k_psi]
 
-    for end in ends:
-        end()
+    @pl.when(summing)
+    def _():
+        wait_bytes(pout.at[pl.ds(0, 2 * n_z - 1)], sum_send_sem.at[2, 1])
+
+    @pl.when(jnp.logical_not(summing))
+    def _():
+        wait_bytes(pout.at[0], pair_send.at[0])
 
 
 def finish(range_in, corange_in, core_in, range_out, corange_out, core_out, sems):
@@ -677,6 +714,7 @@
                 pltpu.SemaphoreType.DMA((2,)),
                 pltpu.SemaphoreType.REGULAR((2,)),
                 pltpu.VMEM((3, coarse, coarse), bf16),
+                pltpu.SemaphoreType.DMA((1,)),
             ],
             compiler_params=pltpu.CompilerParams(
                 collective_id=0, has_side_effects=True

time: 57.1 us -> 56.7 us (level)
  no operation moved by 1% of the time
where the time goes in v4:
time: 56.7 us; the launch traced here: 56.5 us
  Pallas kernels  55.9 us (99%)
  between operations  0.64 us (1%)
    pallas_call x1, Pallas kernels, body(): call(sources[0], diagonal, coarse_ids, coarse_inverse, omega_rows, psi.re...  55.1 us

profile of v4, /device:TPU:1, one launch (start us, length us, event | category | flops | bytes accessed | tf_op | source)
XLA Modules:
  0.0 56.5 jit_solution(130683035450348349)
XLA Ops:
  0.6 55.1 %two_level_sketch.1 = (f32[32,32,128]{2,1,0:T(8,128)S(1)}, f32[4,32]{1,0:T(4,128)S(1)}, f32[64,64]{1,0:T(8,128)S(1)}) custom-call(f32[4,8,512]{2,1,0:T(8,128)} %bitcast.10, f32[4,8,512]{2,1,0:T(8,128)} %diagonal_hbm.1, s32[4,8,512]{2,1,0:T(8,128)} %ids_hbm.1, f32[256,256]{1,0:T(8,128)} %inverse_hbm.1, f32[4,32]{1,0:T(4,128)} %omega_hbm.1, ...), custom_call_target="tpu_custom_call" | custom-call | tf_op jit(solution)/shard_map/two_level_sketch/pallas_call | solution.py:724
  55.7 0.8 %finish.1 = (f32[32,32,128]{2,1,0:T(8,128)}, f32[4,32]{1,0:T(4,128)}, f32[64,64]{1,0:T(8,128)}) custom-call(f32[32,32,128]{2,1,0:T(8,128)S(1)} %get-tuple-element.9.range_in, f32[4,32]{1,0:T(4,128)S(1)} %get-tuple-element.10.corange_in, f32[64,64]{1,0:T(8,128)S(1)} %get-tuple-element.11.core_in), custom_call_target="tpu_custom_call" | custom-call | tf_op jit(solution)/shard_map/finish/pallas_call | solution.py:736

commit v5 on v4

--- a/solution.py
+++ b/solution.py
@@ -406,10 +406,12 @@
                 picked = jnp.where(rank_y_wide == float(b), jnp.broadcast_to(line, wide), picked)
             by_x.append(picked)
         for r in range(n_ext):
-            picked = jnp.zeros(wide, f32)
+            height = rows_y if r in (0, n_ext - 1) else 2 * rows_y
+            picked = jnp.zeros((height, cells_z), f32)
             for a in range(XY_CUTS):
-                picked = jnp.where(rank_x_wide[r] == float(a), by_x[a], picked)
-            store(r, picked)
+                here = rank_x_wide[r][:height] == float(a)
+                picked = jnp.where(here, by_x[a][:height], picked)
+            store(r, pl.ds(0, height), picked)
 
     def sweep(old, new, r):
         here = old[r]
@@ -424,6 +426,9 @@
             for r in range(1 + s, n_ext - 1 - s):
                 if s == SWEEPS - 1:
                     last(r, fields[s % 2])
+                elif r in (1 + s, n_ext - 2 - s):
+                    value = last_value(r, fields[s % 2])
+                    fields[1 - s % 2][r, pl.ds(0, rows_y), :] = value
                 else:
                     sweep(fields[s % 2], fields[1 - s % 2], r)
 
@@ -438,8 +443,8 @@
         own = pl.ds(0, rows_y)
         return here * THIRD + weighted_q[r, own, :] + weight[r, own, :] * around
 
-    def store_first(r, picked):
-        field_a[r] = picked
+    def store_first(r, rows, picked):
+        field_a[r, rows, :] = picked
 
     rhs = end_sum(0)
     correct(rhs, store_first)
@@ -470,9 +475,10 @@
     for copy in halo_copies[pressure_copies:]:
         copy.wait_recv()
 
-    def store_second(r, picked):
-        here = (rank_x_wide[r] >= 0.0) & (rank_y_wide >= 0.0)
-        field_a[r] = picked + jnp.where(here, ext_p[r], 0.0)
+    def store_second(r, rows, picked):
+        height = picked.shape[0]
+        here = (rank_x_wide[r][:height] >= 0.0) & (rank_y_wide[:height] >= 0.0)
+        field_a[r, rows, :] = picked + jnp.where(here, ext_p[r, rows, :], 0.0)
 
     rhs = end_sum(1)
     correct(rhs, store_second)
@@ -511,7 +517,7 @@
             return tuple(out)
 
         zeros = tuple(jnp.zeros((8, LANES), f32) for _ in range(k_all // 8 * n_far))
-        sums = lax.fori_loop(0, per_k, step, zeros)
+        sums = lax.fori_loop(0, per_k, step, zeros, unroll=4)
         for kt in range(k_all // 8):
             for t in range(n_far):
                 to = pl.multiple_of((base + t) * k_all, 8) + kt * 8

time: 56.7 us -> 56.5 us (level)
  no operation moved by 1% of the time
where the time goes in v5:
time: 56.5 us; the launch traced here: 56.3 us
  Pallas kernels  55.7 us (99%)
  between operations  0.64 us (1%)
    pallas_call x1, Pallas kernels, body(): call(sources[0], diagonal, coarse_ids, coarse_inverse, omega_rows, psi.re...  54.8 us

profile of v5, /device:TPU:1, one launch (start us, length us, event | category | flops | bytes accessed | tf_op | source)
XLA Modules:
  0.0 56.3 jit_solution(2755340489165798074)
XLA Ops:
  0.6 54.8 %two_level_sketch.1 = (f32[32,32,128]{2,1,0:T(8,128)S(1)}, f32[4,32]{1,0:T(4,128)S(1)}, f32[64,64]{1,0:T(8,128)S(1)}) custom-call(f32[4,8,512]{2,1,0:T(8,128)} %bitcast.10, f32[4,8,512]{2,1,0:T(8,128)} %diagonal_hbm.1, s32[4,8,512]{2,1,0:T(8,128)} %ids_hbm.1, f32[256,256]{1,0:T(8,128)} %inverse_hbm.1, f32[4,32]{1,0:T(4,128)} %omega_hbm.1, ...), custom_call_target="tpu_custom_call" | custom-call | tf_op jit(solution)/shard_map/two_level_sketch/pallas_call | solution.py:730
  55.5 0.8 %finish.1 = (f32[32,32,128]{2,1,0:T(8,128)}, f32[4,32]{1,0:T(4,128)}, f32[64,64]{1,0:T(8,128)}) custom-call(f32[32,32,128]{2,1,0:T(8,128)S(1)} %get-tuple-element.9.range_in, f32[4,32]{1,0:T(4,128)S(1)} %get-tuple-element.10.corange_in, f32[64,64]{1,0:T(8,128)S(1)} %get-tuple-element.11.core_in), custom_call_target="tpu_custom_call" | custom-call | tf_op jit(solution)/shard_map/finish/pallas_call | solution.py:742
